TPU v7x, 128 devices: a whole 4x4x4 slice. The times are simulated.
128 devices in a mesh: plane: 8 (over z_hi, x), tile: 16 (over z_lo, y, core).
Axes of the slice: x: 4, y: 4, z: 4 (z_hi: 2, z_lo: 2; z = z_hi * 2 + z_lo), core: 2. Of those that a mesh axis runs over, the one named last changes fastest.
Arguments:
- visibility: float32 [2, 262144], P(None, ('plane', 'tile')), may hold values from -6 to 6
- target: int32 [262144, 1], P(('plane', 'tile')), may hold values from 0 to 127; in each aligned block of 2048 rows (0 to 2047, 2048 to 4095, ...) at most 32 rows name the same one
- offset: int32 [262144], P(('plane', 'tile')), may hold values from 0 to 1048575
- taps: float32 [8], replicated, may hold values from 0.1 to 1
- w_plane: float32 [8], P('plane'), may hold values from -300 to 300
Outputs:
- dirty_image: float32 [4096, 4096], P('plane', 'tile')
Inputs may be any that keep to these rules, and one draw needn't show every extreme that they name: `target`: among the rows of one device no value occurs more than 32 times, and some value occurs exactly 32 times.
All inputs are finite; a program needn't handle non-finite values.
Results may differ from a plain program's by a relative error of at most 0.0042.
Values sent between devices are 32-bit elements; how exact they have to be, the bound alone decides.
A program may use at most 128 MiB of HBM per device.

v0:
```python
import math

import jax
import jax.numpy as jnp
from jax import lax
from jax.sharding import Mesh
from jax.sharding import PartitionSpec as P

G = 4096
TILE = ("tile_0", "tile_1", "tile_2")
PLANE = ("plane_0", "plane_1")
PLANE_TILE = ("plane_0", "plane_1", "tile_0", "tile_1", "tile_2")


HIGHEST = lax.Precision.HIGHEST


def split_up(x, dim, length):
    dims = x.shape
    blocks = x.reshape(*dims[:dim], length, dims[dim] // length, *dims[dim + 1 :])
    return jnp.moveaxis(blocks, dim, 0)


def joined_along(blocks, dim):
    blocks = jnp.moveaxis(blocks, 0, dim)
    dims = blocks.shape
    return blocks.reshape(*dims[:dim], dims[dim] * dims[dim + 1], *dims[dim + 2 :])


def moved_by_axis(blocks, axes, sequence):
    dims = [lax.axis_size(a) for a in axes]
    blocks = blocks.reshape(*dims, *blocks.shape[1:])
    for k in sequence:
        blocks = lax.all_to_all(blocks, axes[k], split_axis=k, concat_axis=k, tiled=True)
    return blocks.reshape(-1, *blocks.shape[len(axes) :])


def exchange_by_chip(x, groups, sequence, split_dim, concat_dim):
    length = lax.axis_size(groups[0]) * lax.axis_size(groups[1])
    blocks = split_up(x, split_dim, length)
    return joined_along(moved_by_axis(blocks, groups, sequence), concat_dim)


def shifted(x, axis, by):
    length = lax.axis_size(axis)
    return lax.ppermute(x, axis, [(i, (i + by) % length) for i in range(length)])


def summed_on_arrival(x, axis, dim):
    blocks = split_up(x, dim, lax.axis_size(axis))
    arrived = lax.all_to_all(blocks, axis, split_axis=0, concat_axis=0, tiled=True)
    return arrived.sum(axis=0)


def direction(index, length):
    return ((index + length // 2) % length - length // 2).astype(jnp.float32) * (0.5 / length)


def angle_table(first, second, length):
    product = (
        jnp.arange(first, dtype=jnp.int32)[:, None]
        * jnp.arange(second, dtype=jnp.int32)[None, :]
        % length
    )
    angles = product.astype(jnp.float32) * (2.0 * math.pi / length)
    return (jnp.cos(angles), jnp.sin(angles))


def split_length(length):
    inner_len = math.gcd(length, 128)
    return (length // inner_len, inner_len)


def transform_last(real_part, imag_part):
    length = real_part.shape[-1]
    outer_len, inner_len = split_length(length)
    real_grid = real_part.reshape(-1, outer_len, inner_len)
    imag_grid = imag_part.reshape(-1, outer_len, inner_len)
    cos_one, sin_one = angle_table(outer_len, outer_len, outer_len)
    first_re = jnp.einsum("rab,ak->rkb", real_grid, cos_one, precision=HIGHEST) - jnp.einsum(
        "rab,ak->rkb", imag_grid, sin_one, precision=HIGHEST
    )
    first_im = jnp.einsum("rab,ak->rkb", real_grid, sin_one, precision=HIGHEST) + jnp.einsum(
        "rab,ak->rkb", imag_grid, cos_one, precision=HIGHEST
    )
    cos_tw, sin_tw = angle_table(outer_len, inner_len, length)
    twist_re = first_re * cos_tw - first_im * sin_tw
    twist_im = first_re * sin_tw + first_im * cos_tw
    cos_two, sin_two = angle_table(inner_len, inner_len, inner_len)
    out_re = jnp.einsum("rkb,bq->rqk", twist_re, cos_two, precision=HIGHEST) - jnp.einsum(
        "rkb,bq->rqk", twist_im, sin_two, precision=HIGHEST
    )
    out_im = jnp.einsum("rkb,bq->rqk", twist_re, sin_two, precision=HIGHEST) + jnp.einsum(
        "rkb,bq->rqk", twist_im, cos_two, precision=HIGHEST
    )
    return (out_re.reshape(-1, length), out_im.reshape(-1, length))


def transform_first(real_part, imag_part):
    length = real_part.shape[0]
    outer_len, inner_len = split_length(length)
    real_grid = real_part.reshape(outer_len, inner_len, -1)
    imag_grid = imag_part.reshape(outer_len, inner_len, -1)
    cos_one, sin_one = angle_table(outer_len, outer_len, outer_len)
    first_re = jnp.einsum("abc,ak->kbc", real_grid, cos_one, precision=HIGHEST) - jnp.einsum(
        "abc,ak->kbc", imag_grid, sin_one, precision=HIGHEST
    )
    first_im = jnp.einsum("abc,ak->kbc", real_grid, sin_one, precision=HIGHEST) + jnp.einsum(
        "abc,ak->kbc", imag_grid, cos_one, precision=HIGHEST
    )
    cos_tw, sin_tw = angle_table(outer_len, inner_len, length)
    twist_re = first_re * cos_tw[:, :, None] - first_im * sin_tw[:, :, None]
    twist_im = first_re * sin_tw[:, :, None] + first_im * cos_tw[:, :, None]
    cos_two, sin_two = angle_table(inner_len, inner_len, inner_len)
    out_re = jnp.einsum("kbc,bq->qkc", twist_re, cos_two, precision=HIGHEST) - jnp.einsum(
        "kbc,bq->qkc", twist_im, sin_two, precision=HIGHEST
    )
    out_im = jnp.einsum("kbc,bq->qkc", twist_re, sin_two, precision=HIGHEST) + jnp.einsum(
        "kbc,bq->qkc", twist_im, cos_two, precision=HIGHEST
    )
    return (out_re.reshape(length, -1), out_im.reshape(length, -1))


def grid_block(received, taps, start, block_len, band_rows, totals):
    piece = lax.dynamic_slice_in_dim(received, start, block_len, 1)
    encoded = jnp.maximum(piece[2].astype(jnp.int32) - 1, 0)
    band_row = encoded // G
    column = encoded % G
    kernel_len = taps.shape[0]
    taps_low = taps.astype(jnp.bfloat16)
    weight_re = (taps[None, :] * piece[0][:, None]).astype(jnp.bfloat16)
    weight_im = (taps[None, :] * piece[1][:, None]).astype(jnp.bfloat16)
    rel_row = jnp.arange(band_rows, dtype=jnp.int32)[None, :] - band_row[:, None]
    rel_col = (jnp.arange(G, dtype=jnp.int32)[None, :] - column[:, None]) % G
    row_re = jnp.zeros((block_len, band_rows), jnp.bfloat16)
    row_im = jnp.zeros((block_len, band_rows), jnp.bfloat16)
    col_table = jnp.zeros((block_len, G), jnp.bfloat16)
    for tap_index in range(kernel_len):
        row_re = jnp.where(rel_row == tap_index, weight_re[:, tap_index : tap_index + 1], row_re)
        row_im = jnp.where(rel_row == tap_index, weight_im[:, tap_index : tap_index + 1], row_im)
        col_table = jnp.where(rel_col == tap_index, taps_low[tap_index], col_table)
    row_table = jnp.concatenate([row_re, row_im], axis=1)
    return totals + lax.dot_general(
        row_table, col_table, (((0,), (0,)), ((), ())), preferred_element_type=jnp.float32
    )


def local(visibility, target, offset, taps, w_plane):
    tiles = lax.axis_size(TILE)
    planes = lax.axis_size(PLANE)
    devices = tiles * planes
    vis_dev = visibility.shape[1]
    capacity = 2 * vis_dev // devices
    slot_total = devices * capacity
    band = G // tiles
    columns = G // tiles
    kernel_len = taps.shape[0]
    band_rows = band + kernel_len - 1
    destination = target[:, 0]
    onehot = (destination[:, None] == jnp.arange(devices, dtype=jnp.int32)[None, :]).astype(
        jnp.int32
    )
    rank = jnp.sum(jnp.cumsum(onehot, axis=0) * onehot, axis=1) - 1
    slot = destination * capacity + rank
    payload = jnp.stack([visibility[0], visibility[1], offset.astype(jnp.float32) + 1.0])
    outgoing = jnp.zeros((3, slot_total), jnp.float32).at[:, slot].set(payload)
    received = exchange_by_chip(
        outgoing, (("plane_0", "plane_1", "tile_0", "tile_1"), "tile_2"), (1, 0), 1, 1
    )
    block_len = min(512, slot_total)
    empty = jnp.zeros((2 * band_rows, G), jnp.float32)

    def grid_step(index, totals):
        return grid_block(received, taps, index * block_len, block_len, band_rows, totals)

    gridded = lax.fori_loop(0, slot_total // block_len, grid_step, empty)
    gridded = gridded.reshape(2, band_rows, G)
    incoming = shifted(gridded[:, band:], TILE, 1)
    grid_band = gridded[:, :band].at[:, : kernel_len - 1].add(incoming)
    col_re, col_im = transform_last(grid_band[0], grid_band[1])
    stacked = jnp.stack([col_re, col_im]).reshape(2, band, tiles, columns)
    exchanged = lax.all_to_all(stacked, TILE, split_axis=2, concat_axis=1, tiled=True)
    item_count = exchanged.shape[3]
    rows_re, rows_im = transform_first(
        exchanged[0].reshape(G, item_count), exchanged[1].reshape(G, item_count)
    )
    image_parts = jnp.stack([rows_re, rows_im]).reshape(2, G, 1, item_count).reshape(2, G, columns)
    line_pos = jnp.arange(G, dtype=jnp.int32)
    column_pos = lax.axis_index(TILE) * columns + jnp.arange(columns, dtype=jnp.int32)
    cos_row = direction(line_pos, G)
    cos_col = direction(column_pos, G)
    n_minus = (
        jnp.sqrt(1.0 - cos_row[:, None] * cos_row[:, None] - cos_col[None, :] * cos_col[None, :])
        - 1.0
    )
    phase = 2.0 * math.pi * w_plane[0] * n_minus
    screened = jnp.cos(phase) * image_parts[0] - jnp.sin(phase) * image_parts[1]
    summed = summed_on_arrival(screened, PLANE, 0)
    return summed * (1.0 / math.sqrt(vis_dev * devices))


def solution(mesh):
    finer = Mesh(
        mesh.devices.reshape(2, 4, 2, 4, 2), ("plane_0", "plane_1", "tile_0", "tile_1", "tile_2")
    )
    return jax.shard_map(
        local,
        mesh=finer,
        in_specs=(P(None, PLANE_TILE), P(PLANE_TILE, None), P(PLANE_TILE), P(), P(PLANE)),
        out_specs=P(PLANE, TILE),
        check_vma=False,
    )
```

profile of v0, /device:TPU:0, one launch (start us, length us, event | category | flops | bytes accessed | tf_op | source)
XLA Modules:
  0.0 554.3 jit_solution(2011988327328630223)
XLA Ops:
  2.8 6.1 %scatter_custom_fusion = f32[3,4096]{0,1:T(8,128)S(1)} fusion(s32[2048]{0:T(1024)S(1)} %bitcast.168, f32[2048,3]{1,0:T(8,128)S(1)} %copy.69, f32[]{:T(128)} %constant.337.clone.1), kind=kCustom, calls=%fused_computation.153 | custom fusion | bytes 49156 | tf_op jit(solution)/shard_map/scatter | solution.py:166
  16.3 11.7 %all-to-all-start.1 = ((f32[64,1,192]{2,1,0:T(1,128)}), f32[64,1,192]{2,1,0:T(1,128)S(1)}, u32[]{:S(2)}, u32[]{:S(2)}) async-start(f32[64,1,192]{2,1,0:T(1,128)} %reshape.301), calls=%async_computation.1 | async-start | bytes 131072 | tf_op jit(solution)/shard_map/all_to_all | solution.py:34
  28.0 9.7 %all-to-all-done.1 = f32[64,1,192]{2,1,0:T(1,128)S(1)} async-done(((f32[64,1,192]{2,1,0:T(1,128)}), f32[64,1,192]{2,1,0:T(1,128)S(1)}, u32[]{:S(2)}, u32[]{:S(2)}) %all-to-all-start.1) | async-done | bytes 49184 | tf_op jit(solution)/shard_map/all_to_all | solution.py:34
  39.0 175.1 %while.18 = (s32[]{:T(128)}, f32[526,4096]{1,0:T(8,128)}, f32[3,4096]{1,0:T(4,128)S(1)}, f32[8]{0:T(128)S(1)}, bf16[8]{0:T(256)(128)(2,1)S(1)}, /*index=5*/s32[]...) while((s32[]{:T(128)}, f32[526,4096]{1,0:T(8,128)}, f32[3,4096]{1,0:T(4,128)S(1)}, ...), condition=%wide.region_5.6_spmd.clone, body=%wide.region_4.5_spmd.clone.sunk | while | flops 2273700864 | bytes 18414876 | solution.py:176
  41.6 17.3 %select_add_fusion.2 = f32[526,4096]{1,0:T(8,128)} fusion(f32[526,4096]{1,0:T(8,128)} %get-tuple-element.356, pred[]{:T(512)S(6)} %compare.38, s32[512]{0:T(512)S(1)} %get-tuple-element.312, bf16[]{:T(256)} %bitcast.130, bf16[]{:T(256)} %bitcast.131, bf16[]{:T(256)} %bitcast.132, bf16[]{:T(256)} %bitcast.133, bf16[]{:T(256)} %bitcast.134, ...), kind=kOutput, calls=%fused_computation.4.clone.1 | convolution fusion | flops 2270310400 | bytes 17776656 | tf_op jit(solution)/shard_map/while/body/eval_jaxpr/dot_general | solution.py:143
  61.6 19.5 %select_add_fusion.2 = f32[526,4096]{1,0:T(8,128)} fusion(f32[526,4096]{1,0:T(8,128)} %get-tuple-element.356, pred[]{:T(512)S(6)} %compare.38, s32[512]{0:T(512)S(1)} %get-tuple-element.312, bf16[]{:T(256)} %bitcast.130, bf16[]{:T(256)} %bitcast.131, bf16[]{:T(256)} %bitcast.132, bf16[]{:T(256)} %bitcast.133, bf16[]{:T(256)} %bitcast.134, ...), kind=kOutput, calls=%fused_computation.4.clone.1 | convolution fusion | flops 2270310400 | bytes 17776656 | tf_op jit(solution)/shard_map/while/body/eval_jaxpr/dot_general | solution.py:143
  83.8 19.5 %select_add_fusion.2 = f32[526,4096]{1,0:T(8,128)} fusion(f32[526,4096]{1,0:T(8,128)} %get-tuple-element.356, pred[]{:T(512)S(6)} %compare.38, s32[512]{0:T(512)S(1)} %get-tuple-element.312, bf16[]{:T(256)} %bitcast.130, bf16[]{:T(256)} %bitcast.131, bf16[]{:T(256)} %bitcast.132, bf16[]{:T(256)} %bitcast.133, bf16[]{:T(256)} %bitcast.134, ...), kind=kOutput, calls=%fused_computation.4.clone.1 | convolution fusion | flops 2270310400 | bytes 17776656 | tf_op jit(solution)/shard_map/while/body/eval_jaxpr/dot_general | solution.py:143
  105.9 19.5 %select_add_fusion.2 = f32[526,4096]{1,0:T(8,128)} fusion(f32[526,4096]{1,0:T(8,128)} %get-tuple-element.356, pred[]{:T(512)S(6)} %compare.38, s32[512]{0:T(512)S(1)} %get-tuple-element.312, bf16[]{:T(256)} %bitcast.130, bf16[]{:T(256)} %bitcast.131, bf16[]{:T(256)} %bitcast.132, bf16[]{:T(256)} %bitcast.133, bf16[]{:T(256)} %bitcast.134, ...), kind=kOutput, calls=%fused_computation.4.clone.1 | convolution fusion | flops 2270310400 | bytes 17776656 | tf_op jit(solution)/shard_map/while/body/eval_jaxpr/dot_general | solution.py:143
  128.1 19.5 %select_add_fusion.2 = f32[526,4096]{1,0:T(8,128)} fusion(f32[526,4096]{1,0:T(8,128)} %get-tuple-element.356, pred[]{:T(512)S(6)} %compare.38, s32[512]{0:T(512)S(1)} %get-tuple-element.312, bf16[]{:T(256)} %bitcast.130, bf16[]{:T(256)} %bitcast.131, bf16[]{:T(256)} %bitcast.132, bf16[]{:T(256)} %bitcast.133, bf16[]{:T(256)} %bitcast.134, ...), kind=kOutput, calls=%fused_computation.4.clone.1 | convolution fusion | flops 2270310400 | bytes 17776656 | tf_op jit(solution)/shard_map/while/body/eval_jaxpr/dot_general | solution.py:143
  150.3 19.5 %select_add_fusion.2 = f32[526,4096]{1,0:T(8,128)} fusion(f32[526,4096]{1,0:T(8,128)} %get-tuple-element.356, pred[]{:T(512)S(6)} %compare.38, s32[512]{0:T(512)S(1)} %get-tuple-element.312, bf16[]{:T(256)} %bitcast.130, bf16[]{:T(256)} %bitcast.131, bf16[]{:T(256)} %bitcast.132, bf16[]{:T(256)} %bitcast.133, bf16[]{:T(256)} %bitcast.134, ...), kind=kOutput, calls=%fused_computation.4.clone.1 | convolution fusion | flops 2270310400 | bytes 17776656 | tf_op jit(solution)/shard_map/while/body/eval_jaxpr/dot_general | solution.py:143
  172.4 19.5 %select_add_fusion.2 = f32[526,4096]{1,0:T(8,128)} fusion(f32[526,4096]{1,0:T(8,128)} %get-tuple-element.356, pred[]{:T(512)S(6)} %compare.38, s32[512]{0:T(512)S(1)} %get-tuple-element.312, bf16[]{:T(256)} %bitcast.130, bf16[]{:T(256)} %bitcast.131, bf16[]{:T(256)} %bitcast.132, bf16[]{:T(256)} %bitcast.133, bf16[]{:T(256)} %bitcast.134, ...), kind=kOutput, calls=%fused_computation.4.clone.1 | convolution fusion | flops 2270310400 | bytes 17776656 | tf_op jit(solution)/shard_map/while/body/eval_jaxpr/dot_general | solution.py:143
  194.6 19.5 %select_add_fusion.2 = f32[526,4096]{1,0:T(8,128)} fusion(f32[526,4096]{1,0:T(8,128)} %get-tuple-element.356, pred[]{:T(512)S(6)} %compare.38, s32[512]{0:T(512)S(1)} %get-tuple-element.312, bf16[]{:T(256)} %bitcast.130, bf16[]{:T(256)} %bitcast.131, bf16[]{:T(256)} %bitcast.132, bf16[]{:T(256)} %bitcast.133, bf16[]{:T(256)} %bitcast.134, ...), kind=kOutput, calls=%fused_computation.4.clone.1 | convolution fusion | flops 2270310400 | bytes 17776656 | tf_op jit(solution)/shard_map/while/body/eval_jaxpr/dot_general | solution.py:143
  214.1 7.6 %reshape.264 = f32[2,263,4096]{2,1,0:T(8,128)} reshape(f32[526,4096]{1,0:T(8,128)} %get-tuple-element.158) | data formatting | bytes 17235968 | tf_op jit(solution)/shard_map/reshape | solution.py:177
  222.8 7.6 %slice.405 = f32[2,256,4096]{2,1,0:T(8,128)} slice(f32[2,263,4096]{2,1,0:T(8,128)} %reshape.264), slice={[0:2], [0:256], [0:4096]} | slice | bytes 16777216 | tf_op jit(solution)/shard_map/slice | solution.py:179
  251.6 5.1 subtract_bitcast_fusion.1
  256.7 6.2 %fusion.84 = f32[128,256,32]{1,0,2:T(8,128)S(1)} fusion(f32[256,32,128]{2,1,0:T(8,128)S(1)} %get-tuple-element.234), kind=kOutput, calls=%fused_computation.135 | convolution fusion | flops 1610842112 | bytes 8388608 | tf_op jit(solution)/shard_map/rkb,bq->rqk/dot_general | solution.py:90
  263.0 6.2 %fusion.82 = f32[128,256,32]{1,0,2:T(8,128)S(1)} fusion(f32[256,32,128]{2,1,0:T(8,128)S(1)} %get-tuple-element.234), kind=kOutput, calls=%fused_computation.133 | convolution fusion | flops 1610842112 | bytes 8388608 | tf_op jit(solution)/shard_map/rkb,bq->rqk/dot_general | solution.py:93
  269.2 6.8 %subtract_bitcast_fusion = f32[256,128,32]{0,1,2:T(8,128)S(1)} fusion(f32[128,256,32]{1,0,2:T(8,128)S(1)} %fusion.84, f32[256,32,128]{2,1,0:T(8,128)S(1)} %get-tuple-element.233), kind=kOutput, calls=%fused_computation.114 | convolution fusion | flops 1611890688 | bytes 12582912 | tf_op jit(solution)/shard_map/rkb,bq->rqk/dot_general | solution.py:90
  278.4 6.1 %add_bitcast_fusion = f32[256,128,32]{0,1,2:T(8,128)S(1)} fusion(f32[128,256,32]{1,0,2:T(8,128)S(1)} %fusion.82, f32[256,32,128]{2,1,0:T(8,128)S(1)} %get-tuple-element.233), kind=kOutput, calls=%fused_computation.113 | convolution fusion | flops 1611890688 | bytes 12582912 | tf_op jit(solution)/shard_map/rkb,bq->rqk/dot_general | solution.py:93
  291.8 5.1 all-to-all-start.2
  297.8 112.0 %all-to-all-done.2 = f32[2,256,16,256]{1,3,0,2:T(8,128)} async-done(((f32[2,256,16,256]{1,3,0,2:T(8,128)}), f32[2,256,16,256]{1,3,0,2:T(8,128)}, u32[]{:S(2)}, u32[]{:S(2)}) %all-to-all-start.2) | async-done | bytes 8388640 | tf_op jit(solution)/shard_map/all_to_all | solution.py:182
  409.8 8.7 %copy.81 = f32[2,256,16,256]{3,1,2,0:T(8,128)} copy(f32[2,256,16,256]{1,3,0,2:T(8,128)} %all-to-all-done.2) | data formatting | bytes 16777216 | tf_op jit(solution)/shard_map/all_to_all | solution.py:182
  422.5 5.9 %fusion.76 = f32[32,128,256]{2,0,1:T(8,128)S(1)} fusion(f32[32,128,256]{2,1,0:T(8,128)S(1)} %bitcast.146), kind=kOutput, calls=%fused_computation.127 | convolution fusion | flops 402667520 | bytes 8388608 | tf_op jit(solution)/shard_map/abc,ak->kbc/dot_general | solution.py:105
  428.4 6.6 %fusion.74 = f32[32,128,256]{2,0,1:T(8,128)S(1)} fusion(f32[32,128,256]{2,1,0:T(8,128)S(1)} %bitcast.147), kind=kOutput, calls=%fused_computation.125 | convolution fusion | flops 402667520 | bytes 8388608 | tf_op jit(solution)/shard_map/abc,ak->kbc/dot_general | solution.py:108
  435.0 6.2 %fusion.94 = f32[32,128,256]{2,0,1:T(8,128)S(1)} fusion(f32[32,128,256]{2,0,1:T(8,128)S(1)} %fusion.76, f32[32,128,256]{2,1,0:T(8,128)S(1)} %bitcast.142), kind=kOutput, calls=%fused_computation.141 | convolution fusion | flops 403716096 | bytes 12582912 | tf_op jit(solution)/shard_map/abc,ak->kbc/dot_general | solution.py:105
  441.1 7.9 %multiply_subtract_fusion = (f32[32,128,256]{2,0,1:T(8,128)S(1)}, f32[32,128,256]{2,0,1:T(8,128)S(1)}) fusion(f32[32,128,256]{2,0,1:T(8,128)S(1)} %fusion.94, f32[32,128]{0,1:T(8,128)S(1)} %copy.87, f32[32,128]{0,1:T(8,128)S(1)} %copy.84, f32[32,128,256]{2,0,1:T(8,128)S(1)} %fusion.74, f32[32,128,256]{2,1,0:T(8,128)S(1)} %bitcast.143), kind=kOutput, calls=%fused_computation.112 | convolution fusion | flops 410007552 | bytes 21004288 | tf_op jit(solution)/shard_map/abc,ak->kbc/dot_general | solution.py:108
  449.1 6.0 %fusion.68 = f32[128,32,256]{2,0,1:T(8,128)S(1)} fusion(f32[32,128,256]{2,0,1:T(8,128)S(1)} %get-tuple-element.232), kind=kOutput, calls=%fused_computation.119 | convolution fusion | flops 1610842112 | bytes 8388608 | tf_op jit(solution)/shard_map/kbc,bq->qkc/dot_general | solution.py:115
  455.1 6.5 %fusion.66 = f32[128,32,256]{2,0,1:T(8,128)S(1)} fusion(f32[32,128,256]{2,0,1:T(8,128)S(1)} %get-tuple-element.232), kind=kOutput, calls=%fused_computation.117 | convolution fusion | flops 1610842112 | bytes 8388608 | tf_op jit(solution)/shard_map/kbc,bq->qkc/dot_general | solution.py:118
  461.6 6.0 %fusion.100 = f32[128,32,256]{2,0,1:T(8,128)S(1)} fusion(f32[128,32,256]{2,0,1:T(8,128)S(1)} %fusion.68, f32[32,128,256]{2,0,1:T(8,128)S(1)} %get-tuple-element.231), kind=kOutput, calls=%fused_computation.143 | convolution fusion | flops 1611890688 | bytes 12582912 | tf_op jit(solution)/shard_map/kbc,bq->qkc/dot_general | solution.py:115
  470.0 6.5 %fusion.103 = f32[128,32,256]{2,0,1:T(8,128)S(1)} fusion(f32[128,32,256]{2,0,1:T(8,128)S(1)} %fusion.66, f32[32,128,256]{2,0,1:T(8,128)S(1)} %get-tuple-element.231), kind=kOutput, calls=%fused_computation.144 | convolution fusion | flops 1611890688 | bytes 12582912 | tf_op jit(solution)/shard_map/kbc,bq->qkc/dot_general | solution.py:118
  479.0 16.9 %fusion.65 = f32[8,512,256]{2,1,0:T(8,128)S(1)} fusion(f32[256]{0:T(256)S(1)} %fusion.179, f32[8,512]{1,0:T(8,128)S(1)} %fusion.141, f32[]{:T(128)} %bitcast, f32[8,512,256]{2,1,0:T(8,128)S(1)} %bitcast.150, f32[8,512,256]{2,1,0:T(8,128)S(1)} %bitcast.149), kind=kLoop, calls=%fused_computation.109 | loop fusion | flops 6291456 | bytes 12600324 | tf_op jit(solution)/shard_map/sub | solution.py:197
  496.0 54.5 %all_to_all.31 = f32[8,512,256]{2,1,0:T(8,128)} all-to-all(f32[8,512,256]{2,1,0:T(8,128)S(1)} %fusion.65), channel_id=1, replica_groups=mesh['plane_0'=2,'plane_1'=4,'tile_0'=2,'tile_1'=4,'tile_2'=2] {'plane_0..., dimensions={0} | all-to-all | bytes 8388608 | tf_op jit(solution)/shard_map/all_to_all | solution.py:51
  (125 shorter events, 76.7 us)
Async XLA Ops:
  0.0 1.7 copy-start
  0.0 2.4 copy-start.3
  0.0 2.4 copy-start.1
  1.7 26.3 %copy-start.2 = (f32[8]{0:T(128)S(1)}, f32[8]{0:T(128)}, u32[]{:S(2)}) copy-start(f32[8]{0:T(128)} %param.12) | copy-start | bytes 100
  16.3 21.5 %all-to-all-start.1 = ((f32[64,1,192]{2,1,0:T(1,128)}), f32[64,1,192]{2,1,0:T(1,128)S(1)}, u32[]{:S(2)}, u32[]{:S(2)}) async-start(f32[64,1,192]{2,1,0:T(1,128)} %reshape.301), calls=%async_computation.1 | async-start | bytes 131072 | tf_op jit(solution)/shard_map/all_to_all | solution.py:34
  222.7 8.0 %collective-permute-start = (f32[2,7,4096]{2,1,0:T(8,128)S(1)}, f32[2,7,4096]{2,1,0:T(8,128)S(1)}, u32[]{:S(2)}, u32[]{:S(2)}) collective-permute-start(f32[2,7,4096]{2,1,0:T(8,128)S(1)} %slice.407), channel_id=1, source_target_pairs={{0,1},{1,2},{2,3},{3,4},{4,5},{5,6},{6,7},{7,8},{8,9},{9,10},{10,1... | collective-permute-start | bytes 688136 | tf_op jit(solution)/shard_map/ppermute | solution.py:46
  291.8 118.0 %all-to-all-start.2 = ((f32[2,256,16,256]{1,3,0,2:T(8,128)}), f32[2,256,16,256]{1,3,0,2:T(8,128)}, u32[]{:S(2)}, u32[]{:S(2)}) async-start(f32[2,256,16,256]{1,3,0,2:T(8,128)} %copy.80), calls=%async_computation.2 | async-start | bytes 16777216 | tf_op jit(solution)/shard_map/all_to_all | solution.py:182
where the time goes:
time: 561 us; the launch traced here: 554 us
  matrix products  248 us (44%)
  waiting for transfers between devices  122 us (22%)
  local copies, waits for them, and re-layouts  67.9 us (12%)
  blocking collectives  58.3 us (10%)
  other arithmetic  39.3 us (7%)
  starting transfers between devices  16.9 us (3%)
    dot_general x8, matrix products, grid_block(): lax.dot_general(row_table, col_table, (((0,), (0,)), ((), ())), preferred...  154 us
    all_to_all x1, waiting for transfers between devices, local(): lax.all_to_all(stacked, TILE, split_axis=2, concat_axis=1, tiled=True)  112 us
    all_to_all x1, blocking collectives, summed_on_arrival(): lax.all_to_all(blocks, axis, split_axis=0, concat_axis=0, tiled=True)  54.5 us
    sub x1, other arithmetic, local(): screened = jnp.cos(phase) * image_parts[0] - jnp.sin(phase) * image_parts[1]  16.9 us
    select_n x8, other arithmetic, grid_block(): jnp.where(rel_row == tap_index, weight_re[:, tap_index:tap_index + 1], ro...  12.7 us
    all_to_all x1, starting transfers between devices, moved_by_axis(): lax.all_to_all(blocks, axes[k], split_axis=k, concat_axis=k, tiled=True)  11.7 us
  transfers between devices with their start and end apart: 3, of which 3 were waited for; matrix products, arithmetic and copies ran while one was open for 1% of the time, Pallas kernels for 0%

commit v1 on v0

v1 whole, which is shorter than its diff:
```python
import math

import jax
import jax.numpy as jnp
import numpy as np
from jax import lax
from jax.experimental import pallas as pl
from jax.experimental.pallas import tpu as pltpu
from jax.sharding import PartitionSpec as P


G = 4096
KS = 8
MESH = pl.DeviceIdType.MESH
F32 = jnp.float32
BF16 = jnp.bfloat16
NT = (((1,), (1,)), ((), ()))

SIN = (3.1415927410125732, -5.167710304260254, 2.550077438354492, -0.598291277885437, 0.07765766233205795)
COS = (0.9999999403953552, -4.934792995452881, 4.058411121368408, -1.331876516342163, 0.21968960762023926)


def poly(coefs, g):
    out = g * coefs[-1] + coefs[-2]
    for c in coefs[-3::-1]:
        out = out * g + c
    return out


def cos_sin(cycles):
    f = cycles - jnp.floor(cycles + 0.5)
    g = f * f
    s = f * poly(SIN, g)
    c = poly(COS, g)
    s2 = s + s
    return 1.0 - s2 * s, s2 * c


def rotated(re, im, c, s):
    return re * c - im * s, re * s + im * c


def sort_kernel(vis_ref, tgt_ref, off_ref, out_ref):
    count = tgt_ref.shape[1]
    blk = 256
    ii = lax.broadcasted_iota(jnp.int32, (blk, blk), 0)
    jj = lax.broadcasted_iota(jnp.int32, (blk, blk), 1)
    tri = jnp.where(ii < jj, 1.0, 0.0).astype(BF16)
    rows = lax.broadcasted_iota(jnp.int32, (128, blk), 0)
    ranks = lax.broadcasted_iota(jnp.int32, (32, blk), 0).astype(F32)
    carry = jnp.zeros((128, 1), F32)
    acc = jnp.zeros((128, 128), F32)
    for b in range(count // blk):
        sl = slice(b * blk, (b + 1) * blk)
        one = jnp.where(rows == tgt_ref[:, sl], 1.0, 0.0)
        oneb = one.astype(BF16)
        before = jnp.dot(oneb, tri, preferred_element_type=F32)
        rank = jnp.sum(one * (before + carry), axis=0, keepdims=True)
        carry = carry + jnp.sum(one, axis=1, keepdims=True)
        hit = ranks == rank
        off = off_ref[:, sl]
        parts = [((off >> 12) << 12).astype(F32), (((off >> 4) & 255) << 4).astype(F32), (off & 15).astype(F32)]
        left = [vis_ref[0:1, sl], vis_ref[1:2, sl]]
        for k in range(3):
            cols = []
            for v in range(2):
                top = left[v].astype(BF16).astype(F32)
                left[v] = left[v] - top
                cols.append(jnp.where(hit, top, 0.0))
            cols.append(jnp.where(hit, parts[k], 0.0))
            cols.append(jnp.zeros((32, blk), F32))
            table = jnp.concatenate(cols, axis=0).astype(BF16)
            acc = acc + lax.dot_general(oneb, table, NT, preferred_element_type=F32)
    out_ref[...] = acc


def sort_call(vis, tgt, off):
    return pl.pallas_call(
        sort_kernel,
        out_shape=jax.ShapeDtypeStruct((128, 128), F32),
        in_specs=[pl.BlockSpec(memory_space=pltpu.VMEM)] * 3,
        out_specs=pl.BlockSpec(memory_space=pltpu.VMEM),
        name="sortvis",
    )(vis, tgt, off)


def place():
    p = lax.axis_index("plane")
    t = lax.axis_index("tile")
    zh, x = p // 4, p % 4
    zl, y, core = t // 8, (t // 2) % 4, t % 2
    return zh, x, zl, y, core


def exchange_kernel(s_ref, w_ref, ga_ref, wo_ref, ra, sa, qa, sy, qy, sz, qz, sc, qc, sw, qw):
    zh, x, zl, y, core = place()
    z = zh * 2 + zl
    p, t = zh * 4 + x, zl * 8 + y * 2 + core

    def at_x(d):
        return {"plane": zh * 4 + (x + d) % 4, "tile": t}

    def at_y(d):
        return {"plane": p, "tile": zl * 8 + ((y + d) % 4) * 2 + core}

    def at_z(d):
        zz = (z + d) % 4
        return {"plane": (zz // 2) * 4 + x, "tile": (zz % 2) * 8 + y * 2 + core}

    partner = {"plane": p, "tile": zl * 8 + y * 2 + (1 - core)}

    barrier = pltpu.get_barrier_semaphore()
    for d in (1, 2, 3):
        for at in (at_x, at_y, at_z):
            pl.semaphore_signal(barrier, inc=1, device_id=at(d), device_id_type=MESH)
    pl.semaphore_signal(barrier, inc=1, device_id=partner, device_id_type=MESH)
    pl.semaphore_wait(barrier, 10)

    def copy(src, dst, send, recv, device):
        c = pltpu.make_async_remote_copy(
            src_ref=src, dst_ref=dst, send_sem=send, recv_sem=recv, device_id=device, device_id_type=MESH
        )
        c.start()
        return c

    first = [copy(s_ref.at[:, (x + d) % 4], ra.at[x], sa.at[d - 1], qa.at[d - 1], at_x(d)) for d in (1, 2, 3)]
    wcopy = copy(w_ref, wo_ref.at[zh], sw, qw, at_z(2))
    wo_ref[zh] = w_ref[...]
    ra[x] = s_ref[:, x]
    for c in first:
        c.wait()
    got = [ra[s].reshape(32, 128) for s in range(4)]
    group = lax.broadcasted_iota(jnp.int32, (32, 128), 1) // 32
    for k in range(3):
        row = jnp.zeros((32, 128), F32)
        for s in range(4):
            shift = (32 * (s - k)) % 128
            moved = pltpu.roll(got[s], shift, 1) if shift else got[s]
            row = jnp.where(group == s, moved, row)
        ga_ref[z, y, core, 0, k] = row[:16]
        ga_ref[z, y, core, 1, k] = row[16:]
    mine = ga_ref.at[z, y, core]
    one_y = [copy(mine.at[0], mine.at[0], sy.at[0, d - 1], qy.at[0, d - 1], at_y(d)) for d in (1, 3, 2)]
    one_z = [copy(mine.at[1], mine.at[1], sz.at[0, d - 1], qz.at[0, d - 1], at_z(d)) for d in (1, 3, 2)]
    for c in one_y:
        c.wait()
    part = ga_ref.at[z, :, core, 0]
    two_z = [copy(part, part, sz.at[1, d - 1], qz.at[1, d - 1], at_z(d)) for d in (1, 3, 2)]
    for c in one_z:
        c.wait()
    part = ga_ref.at[:, y, core, 1]
    two_y = [copy(part, part, sy.at[1, d - 1], qy.at[1, d - 1], at_y(d)) for d in (1, 3, 2)]
    for c in two_z:
        c.wait()
    part = ga_ref.at[:, :, core, 0]
    last = [copy(part, part, sc.at[0], qc.at[0], partner)]
    for c in two_y:
        c.wait()
    part = ga_ref.at[:, :, core, 1]
    last.append(copy(part, part, sc.at[1], qc.at[1], partner))
    wcopy.wait()
    for c in last:
        c.wait()


def exchange_call(s, w):
    dma = pltpu.SemaphoreType.DMA
    return pl.pallas_call(
        exchange_kernel,
        out_shape=(jax.ShapeDtypeStruct((4, 4, 2, 2, 3, 16, 128), F32), jax.ShapeDtypeStruct((2, 8, 128), F32)),
        in_specs=[pl.BlockSpec(memory_space=pltpu.VMEM)] * 2,
        out_specs=(pl.BlockSpec(memory_space=pltpu.VMEM),) * 2,
        scratch_shapes=[
            pltpu.VMEM((4, 2, 16, 128), F32),
            dma((3,)),
            dma((3,)),
            dma((2, 3)),
            dma((2, 3)),
            dma((2, 3)),
            dma((2, 3)),
            dma((2,)),
            dma((2,)),
            dma,
            dma,
        ],
        compiler_params=pltpu.CompilerParams(collective_id=0, has_side_effects=True),
        name="exchangevis",
    )(s, w)


def dft(re, im):
    n = len(re)
    if n == 1:
        return re, im
    er, ei = dft(re[0::2], im[0::2])
    dr, di = dft(re[1::2], im[1::2])
    h = n // 2
    out_r, out_i = [None] * n, [None] * n
    for k in range(h):
        if k == 0:
            tr, ti = dr[k], di[k]
        elif 4 * k == n:
            tr, ti = -di[k], dr[k]
        elif 8 * k == n:
            q = math.sqrt(0.5)
            tr, ti = (dr[k] - di[k]) * q, (dr[k] + di[k]) * q
        elif 8 * k == 3 * n:
            q = math.sqrt(0.5)
            tr, ti = (dr[k] + di[k]) * -q, (dr[k] - di[k]) * q
        else:
            c, s = math.cos(2 * math.pi * k / n), math.sin(2 * math.pi * k / n)
            tr, ti = dr[k] * c - di[k] * s, dr[k] * s + di[k] * c
        out_r[k], out_i[k] = er[k] + tr, ei[k] + ti
        out_r[k + h], out_i[k + h] = er[k] - tr, ei[k] - ti
    return out_r, out_i


def grid_kernel(mb_ref, ga_ref, tw_ref, out_ref, hs, xs, ts, rs, iota, *bufs):
    tabs, hots = bufs[:4], bufs[4:]
    mb = mb_ref[0]
    iota[...] = lax.broadcasted_iota(jnp.int32, (256, 128), 0).astype(F32).astype(BF16)

    def fill(zh, band, g):
        start = g * 8 * 96 + zh * 48 + band
        re = ga_ref[pl.ds(start, 8, stride=96), :]
        im = ga_ref[pl.ds(start + 16, 8, stride=96), :]
        off = ga_ref[pl.ds(start + 32, 8, stride=96), :]
        row = jnp.floor(off * (1.0 / G))
        col = off - row * G
        cb, sb = cos_sin(col * mb * (1.0 / G))
        c1, s1 = cos_sin(col * (1.0 / G))
        c8, s8 = cos_sin(col * (8.0 / G))
        re, im = rotated(re, im, cb, sb)
        for s in range(8):
            nr, ni = rotated(re, im, c8, s8)
            xs[g, 0, s * 8 : s * 8 + 8] = re
            xs[g, 1, s * 8 : s * 8 + 8] = im
            xs[g, 2, s * 8 : s * 8 + 8] = nr
            xs[g, 3, s * 8 : s * 8 + 8] = ni
            if s < 7:
                re, im = rotated(re, im, c1, s1)
        ts[g] = c8 + c8
        rs[g] = row
        tab, hot = tabs[g], hots[g]
        for dev in range(8):
            lanes = slice(dev * 128, dev * 128 + 128)
            t = jnp.broadcast_to(ts[g, dev : dev + 1, :], (8, 128))
            for v in range(2):
                a = xs[g, v, pl.ds(dev, 8, stride=8), :]
                b = xs[g, 2 + v, pl.ds(dev, 8, stride=8), :]
                for k in range(0, 16, 2):
                    tab[v * 128 + k * 8 : v * 128 + k * 8 + 16, lanes] = jnp.concatenate([a, b], axis=0).astype(BF16)
                    if k < 14:
                        a = t * b - a
                        b = t * a - b
            r = jnp.broadcast_to(rs[g, dev : dev + 1, :], (16, 128)).astype(BF16)
            for j in range(16):
                hot[j * 16 : j * 16 + 16, lanes] = jnp.where(
                    iota[j * 16 : j * 16 + 16] == r, jnp.ones((), BF16), jnp.zeros((), BF16)
                )

    def product(g):
        return lax.dot_general(tabs[g][...], hots[g][...], NT, preferred_element_type=F32)

    def plane(zh, _):
        def bands(band, _):
            for g in range(4):
                fill(zh, band, g)
            acc = product(0)
            for g in range(1, 4):
                acc = acc + product(g)
            hs[band] = acc
            return 0

        lax.fori_loop(0, 16, bands, 0)

        def strip(i, _):
            m = pl.multiple_of(i * 16, 16)
            for h in range(2):
                lanes = slice(h * 128, h * 128 + 128)
                re = [hs[b, pl.ds(m, 16), lanes] for b in range(16)]
                im = [hs[b, pl.ds(m + 128, 16), lanes] for b in range(16)]
                re, im = dft(re, im)
                for q in range(16):
                    a, b = re[q], im[q]
                    if q:
                        a, b = rotated(a, b, tw_ref[0, q : q + 1, lanes], tw_ref[1, q : q + 1, lanes])
                    out_ref[zh, q, pl.ds(m, 16), lanes] = a.astype(BF16)
                    out_ref[zh, q, pl.ds(m + 128, 16), lanes] = b.astype(BF16)
            return 0

        lax.fori_loop(0, 8, strip, 0)
        return 0

    lax.fori_loop(0, 2, plane, 0)


def grid_call(mb, ga, tw):
    vmem = pl.BlockSpec(memory_space=pltpu.VMEM)
    return pl.pallas_call(
        grid_kernel,
        out_shape=jax.ShapeDtypeStruct((2, 16, 256, 256), BF16),
        in_specs=[pl.BlockSpec(memory_space=pltpu.SMEM), vmem, vmem],
        out_specs=vmem,
        scratch_shapes=[
            pltpu.VMEM((16, 256, 256), F32),
            pltpu.VMEM((4, 4, 64, 128), F32),
            pltpu.VMEM((4, 8, 128), F32),
            pltpu.VMEM((4, 8, 128), F32),
            pltpu.VMEM((256, 128), BF16),
        ]
        + [pltpu.VMEM((256, 1024), BF16)] * 8,
        compiler_params=pltpu.CompilerParams(vmem_limit_bytes=32 << 20),
        name="gridvis",
    )(mb, ga, tw)


def image_kernel(ab_ref, hp_ref, w_ref, dm_ref, out_ref, sr, si, pb, r1, fw, rc, rd, zb, zr, *sems):
    s1, q1, sf, qf, sd, qd, sz, qz = sems
    zh, x, zl, y, core = place()
    t = zl * 8 + y * 2 + core
    xp, xm = (x + 1) % 4, (x + 3) % 4
    right, left = {"plane": zh * 4 + xp, "tile": t}, {"plane": zh * 4 + xm, "tile": t}
    across = {"plane": (1 - zh) * 4 + x, "tile": t}

    barrier = pltpu.get_barrier_semaphore()
    for dev in (right, left, across):
        pl.semaphore_signal(barrier, inc=1, device_id=dev, device_id_type=MESH)

    l0 = lax.broadcasted_iota(jnp.int32, (256, 128), 0)
    lane = lax.broadcasted_iota(jnp.int32, (256, 128), 1)
    ec, es = cos_sin((l0 * 16 + lane).astype(F32) * (1.0 / G))
    ar, ai = jnp.full((256, 128), ab_ref[0, KS - 1]), jnp.zeros((256, 128), F32)
    for j in range(KS - 2, -1, -1):
        ar, ai = rotated(ar, ai, ec, es)
        ar = ar + ab_ref[0, j]
    sr[...] = ar
    si[...] = ai
    m = t * 256 + zh * 128 + lax.broadcasted_iota(jnp.int32, (8, 128), 1)
    ec, es = cos_sin(m.astype(F32) * (1.0 / G))
    tr, ti = jnp.full((8, 128), ab_ref[1, KS - 1]), jnp.zeros((8, 128), F32)
    for j in range(KS - 2, -1, -1):
        tr, ti = rotated(tr, ti, ec, es)
        tr = tr + ab_ref[1, j]
    tr, ti = tr[0:1] * (1.0 / 512.0), ti[0:1] * (1.0 / 512.0)
    ym = jnp.where(m >= G // 2, m - G, m).astype(F32)[0:1] * (0.5 / G)
    ysq = ym * ym
    ws = [w_ref[q, 0:1, :] for q in range(2)]
    row = lax.broadcasted_iota(jnp.int32, (64, 128), 0)

    pl.semaphore_wait(barrier, 3)

    def copy(src, dst, send, recv, device):
        return pltpu.make_async_remote_copy(
            src_ref=src, dst_ref=dst, send_sem=send, recv_sem=recv, device_id=device, device_id_type=MESH
        )

    def step_one(i):
        xo = (x + 2) % 4
        return (
            copy(pb.at[i, 0, xo], r1.at[i, 0], s1.at[i, 0], q1.at[i, 0], right),
            copy(pb.at[i, 1, xo], r1.at[i, 1], s1.at[i, 1], q1.at[i, 1], left),
        )

    def direct(i):
        return (
            copy(pb.at[i, 0, xm], rd.at[i, 0], sd.at[i, 0], qd.at[i, 0], left),
            copy(pb.at[i, 1, xp], rd.at[i, 1], sd.at[i, 1], qd.at[i, 1], right),
        )

    def forward(i):
        return (
            copy(fw.at[i, 0], rc.at[i, 0], sf.at[i, 0], qf.at[i, 0], right),
            copy(fw.at[i, 1], rc.at[i, 1], sf.at[i, 1], qf.at[i, 1], left),
        )

    def over(i):
        return copy(zb.at[i], zr.at[i], sz.at[i], qz.at[i], across)

    def compute(i):
        for q in range(4):
            rows = slice(q * 64, q * 64 + 64)
            l = (row + q * 64) * 16 + i
            xl = jnp.where(l >= G // 2, l - G, l).astype(F32) * (0.5 / G)
            rho = xl * xl + ysq
            n = -rho / (1.0 + jnp.sqrt(1.0 - rho))
            zre = zim = None
            for v in range(2):
                hp = hp_ref[v, i]
                pc = lax.dot_general(dm_ref[rows, :], hp, NT, preferred_element_type=F32)
                ps = lax.dot_general(dm_ref[256 + q * 64 : 320 + q * 64, :], hp, NT, preferred_element_type=F32)
                dre = pc[:, :128] - ps[:, 128:]
                dim = ps[:, :128] + pc[:, 128:]
                c, s = cos_sin(ws[v] * n)
                a, b = rotated(dre, dim, c, s)
                zre, zim = (a, b) if zre is None else (zre + a, zim + b)
            a, b = rotated(zre, zim, tr, ti)
            lanes = lax.broadcasted_iota(jnp.int32, (64, 128), 1)
            cs = jnp.sum(jnp.where(lanes == i, sr[rows], 0.0), axis=1, keepdims=True)
            ss = jnp.sum(jnp.where(lanes == i, si[rows], 0.0), axis=1, keepdims=True)
            part = cs * a - ss * b
            for k in range(2):
                pb[i, q // 2, (q % 2) * 2 + k] = part[k * 32 : k * 32 + 32]

    def put(i, half, value):
        out_ref[pl.ds(half * 512 + i, 32, stride=16), :] = value

    lag1, lag2, lag3 = 1, 3, 5

    def turn(i, _):
        @pl.when(i < 16)
        def _():
            compute(i)
            for c in step_one(i) + direct(i):
                c.start()

        @pl.when(jnp.logical_and(i >= lag1, i < 16 + lag1))
        def _():
            j = i - lag1
            for c in step_one(j):
                c.wait_recv()
            fw[j, 0] = r1[j, 0] + pb[j, 0, xp]
            fw[j, 1] = r1[j, 1] + pb[j, 1, xm]
            for c in forward(j):
                c.start()

        @pl.when(jnp.logical_and(i >= lag2, i < 16 + lag2))
        def _():
            j = i - lag2
            for c in forward(j) + direct(j):
                c.wait_recv()
            put(j, zh, pb[j, zh, x] + rc[j, zh] + rd[j, zh])
            zb[j] = pb[j, 1 - zh, x] + rc[j, 1 - zh] + rd[j, 1 - zh]
            over(j).start()

        @pl.when(i >= lag3)
        def _():
            j = i - lag3
            over(j).wait_recv()
            put(j, 1 - zh, zr[j])

        return 0

    lax.fori_loop(0, 16 + lag3, turn, 0)

    def drain(i, _):
        for c in step_one(i) + direct(i) + forward(i) + (over(i),):
            c.wait_send()
        return 0

    lax.fori_loop(0, 16, drain, 0)


def image_call(ab, hp, w, dm):
    dma = pltpu.SemaphoreType.DMA
    vmem = pl.BlockSpec(memory_space=pltpu.VMEM)
    buf = pltpu.VMEM((16, 2, 32, 128), F32)
    half = pltpu.VMEM((16, 32, 128), F32)
    return pl.pallas_call(
        image_kernel,
        out_shape=jax.ShapeDtypeStruct((1024, 128), F32),
        in_specs=[pl.BlockSpec(memory_space=pltpu.SMEM), vmem, vmem, vmem],
        out_specs=vmem,
        scratch_shapes=[pltpu.VMEM((256, 128), F32)] * 2
        + [pltpu.VMEM((16, 2, 4, 32, 128), F32), buf, buf, buf, buf, half, half]
        + [dma((16, 2))] * 6
        + [dma((16,))] * 2,
        compiler_params=pltpu.CompilerParams(collective_id=1, has_side_effects=True, vmem_limit_bytes=32 << 20),
        name="imagesum",
    )(ab, hp, w, dm)


def constants():
    k = np.arange(256)
    a = 2 * np.pi * (np.outer(k, k) % 256) / 256
    dm = np.concatenate([np.cos(a), np.sin(a)], axis=0)
    b = 2 * np.pi * np.outer(np.arange(16), k) / G
    return dm.astype(jnp.bfloat16), np.stack([np.cos(b), np.sin(b)]).astype(np.float32)


def local(visibility, target, offset, taps, w_plane):
    dm, tw = constants()
    count = visibility.shape[1]
    s = sort_call(visibility, target.reshape(1, count), offset.reshape(1, count))
    w = jnp.broadcast_to(w_plane.reshape(1, 1), (8, 128))
    ga, wo = exchange_call(s.reshape(2, 4, 16, 128), w)
    mb = lax.axis_index("tile") * 256 + (lax.axis_index("plane") // 4) * 128
    hp = grid_call(mb.astype(F32).reshape(1), ga.reshape(32 * 96, 128), jnp.asarray(tw))
    ab = jnp.stack([taps, taps.astype(BF16).astype(F32)])
    halves = image_call(ab, hp, wo, jnp.asarray(dm))
    return jnp.concatenate([halves[:512], halves[512:]], axis=1)


def solution(mesh):
    planes, tiles = ("plane",), ("tile",)
    both = planes + tiles
    return jax.shard_map(
        local,
        mesh=mesh,
        in_specs=(P(None, both), P(both, None), P(both), P(), P("plane")),
        out_specs=P("plane", "tile"),
        check_vma=False,
    )
```

time: 561 us -> 129 us (0.23); the launches traced: 554 us -> 128 us
  matrix products: 248 us -> 0 us
  Pallas kernels: 0 us -> 124 us
  waiting for transfers between devices: 122 us -> 0 us
  local copies, waits for them, and re-layouts: 67.9 us -> 2.8 us
  blocking collectives: 58.3 us -> 0 us
  other arithmetic: 39.3 us -> 0.84 us
  starting transfers between devices: 16.9 us -> 0 us
    dot_general x24 -> x0, matrix products: 248 us -> none  [the longest x8 154 us: grid_block(): lax.dot_general(row_table, col_table, (((0,), (0,)), ((), ())), preferred...]
    pallas_call x0 -> x4, Pallas kernels: none -> 124 us  [the longest x1 50.7 us: grid_call(): pl.pallas_call(grid_kernel, out_shape=jax.ShapeDtypeStruct((2, 16, 256, 2...]
    all_to_all x2 -> x0, waiting for transfers between devices: 122 us -> none  [the longest x1 112 us: local(): lax.all_to_all(stacked, TILE, split_axis=2, concat_axis=1, tiled=True)]
    all_to_all x2 -> x0, blocking collectives: 58.3 us -> none  [the longest x1 54.5 us: summed_on_arrival(): lax.all_to_all(blocks, axis, split_axis=0, concat_axis=0, tiled=True)]
    slice x27 -> x1, local copies, waits for them, and re-layouts: 19.4 us -> 0.04 us  [local(): return jnp.concatenate([halves[:512], halves[512:]], axis=1)]
    sub x3 -> x0, other arithmetic: 17 us -> none  [the longest x1 16.9 us: local(): screened = jnp.cos(phase) * image_parts[0] - jnp.sin(phase) * image_parts[1]]
    all_to_all x2 -> x0, starting transfers between devices: 16.8 us -> none  [the longest x1 11.7 us: moved_by_axis(): lax.all_to_all(blocks, axes[k], split_axis=k, concat_axis=k, tiled=True)]
    select_n x17 -> x0, other arithmetic: 12.8 us -> none  [the longest x8 12.7 us: grid_block(): jnp.where(rel_row == tap_index, weight_re[:, tap_index:tap_index + 1], ro...]
  transfers between devices with their start and end apart: 3 -> 0, of which waited for: 3 -> 0; matrix products, arithmetic and copies ran while one was open for 1% -> 0% of each run, Pallas kernels for 0% -> 0%
where the time goes in v1:
time: 129 us; the launch traced here: 128 us
  Pallas kernels  124 us (96%)
  local copies, waits for them, and re-layouts  2.8 us (2%)
    pallas_call x1, Pallas kernels, grid_call(): pl.pallas_call(grid_kernel, out_shape=jax.ShapeDtypeStruct((2, 16, 256, 2...  50.7 us
    pallas_call x1, Pallas kernels, image_call(): pl.pallas_call(image_kernel, out_shape=jax.ShapeDtypeStruct((1024, 128),...  46.4 us
    pallas_call x1, Pallas kernels, exchange_call(): pl.pallas_call(exchange_kernel, out_shape=(jax.ShapeDtypeStruct((4, 4, 2,...  23.8 us
    pallas_call x1, Pallas kernels, sort_call(): pl.pallas_call(sort_kernel, out_shape=jax.ShapeDtypeStruct((128, 128), F3...  3.05 us

profile of v1, /device:TPU:0, one launch (start us, length us, event | category | flops | bytes accessed | tf_op | source)
XLA Modules:
  0.0 128.3 jit_solution(9590377927855767631)
XLA Ops:
  0.0 0.0 copy-start.4
  0.0 3.0 %sortvis.1 = f32[128,128]{1,0:T(8,128)} custom-call(f32[2,2048]{1,0:T(2,128)} %vis_ref.1, s32[1,2048]{1,0:T(1,128)} %bitcast.13, s32[1,2048]{1,0:T(1,128)} %bitcast.14), custom_call_target="tpu_custom_call" | custom-call | tf_op jit(solution)/shard_map/sortvis/pallas_call | solution.py:78
  3.7 0.6 broadcast_in_dim.8.w_ref
  4.3 23.8 %exchangevis.1 = (f32[4,4,2,2,3,16,128]{6,5,4,3,2,1,0:T(8,128)}, f32[2,8,128]{2,1,0:T(8,128)}) custom-call(f32[2,4,16,128]{3,2,1,0:T(8,128)} %bitcast.12, f32[8,128]{1,0:T(8,128)} %broadcast_in_dim.8.w_ref), custom_call_target="tpu_custom_call" | custom-call | tf_op jit(solution)/shard_map/exchangevis/pallas_call | solution.py:168
  28.1 0.0 copy-start
  28.1 1.4 %copy-done = f32[4,4,2,2,3,16,128]{6,5,4,3,2,1,0:T(8,128)S(1)} copy-done((f32[4,4,2,2,3,16,128]{6,5,4,3,2,1,0:T(8,128)S(1)}, f32[4,4,2,2,3,16,128]{6,5,4,3,2,1,0:T(8,128)}, u32[]{:S(2)}) %copy-start) | copy-done | bytes 1572888
  29.5 0.0 copy-start.2
  29.5 0.8 copy-done.2
  30.2 0.0 copy-start.1
  30.2 0.0 copy-start.3
  30.2 50.7 %gridvis.1.hp_ref = bf16[2,16,256,256]{3,2,1,0:T(8,128)(2,1)S(1)} custom-call(f32[1]{0:T(128)} %bitcast.2.mb_ref, f32[3072,128]{1,0:T(8,128)S(1)} %bitcast.11, f32[2,16,256]{2,1,0:T(8,128)S(1)} %copy-done.2), custom_call_target="tpu_custom_call" | custom-call | tf_op jit(solution)/shard_map/gridvis/pallas_call | solution.py:300
  81.0 0.0 copy-done.4
  81.0 0.0 copy-done.1
  81.0 0.0 copy-done.3
  81.0 46.4 %imagesum.1 = f32[1024,128]{1,0:T(8,128)S(1)} custom-call(f32[2,8]{1,0:T(2,128)S(1)} %pad_maximum_fusion.1.ab_ref, bf16[2,16,256,256]{3,2,1,0:T(8,128)(2,1)S(1)} %gridvis.1.hp_ref, f32[2,8,128]{2,1,0:T(8,128)S(1)} %copy-done.3, bf16[512,256]{1,0:T(8,128)(2,1)S(1)} %copy-done.1), custom_call_target="tpu_custom_call" | custom-call | tf_op jit(solution)/shard_map/imagesum/pallas_call | solution.py:459
  127.4 0.8 pad_maximum_fusion
  (3 shorter events, 0.0 us)
Async XLA Ops:
  0.0 81.0 %copy-start.4 = (f32[8]{0:T(128)S(1)}, f32[8]{0:T(128)}, u32[]{:S(2)}) copy-start(f32[8]{0:T(128)} %param.10) | copy-start | bytes 100
  28.1 1.4 %copy-start = (f32[4,4,2,2,3,16,128]{6,5,4,3,2,1,0:T(8,128)S(1)}, f32[4,4,2,2,3,16,128]{6,5,4,3,2,1,0:T(8,128)}, u32[]{:S(2)}) copy-start(f32[4,4,2,2,3,16,128]{6,5,4,3,2,1,0:T(8,128)} %get-tuple-element.7) | copy-start | bytes 4718596
  29.5 0.8 copy-start.2
  30.2 50.8 %copy-start.1 = (bf16[512,256]{1,0:T(8,128)(2,1)S(1)}, bf16[512,256]{1,0:T(8,128)(2,1)}, u32[]{:S(2)}) copy-start(bf16[512,256]{1,0:T(8,128)(2,1)} %constant.34.clone.dm_ref) | copy-start | bytes 786436
  30.2 50.8 %copy-start.3 = (f32[2,8,128]{2,1,0:T(8,128)S(1)}, f32[2,8,128]{2,1,0:T(8,128)}, u32[]{:S(2)}) copy-start(f32[2,8,128]{2,1,0:T(8,128)} %get-tuple-element.8.w_ref) | copy-start | bytes 24580

commit v2 on v1

--- a/solution.py
+++ b/solution.py
@@ -215,10 +215,10 @@
     return out_r, out_i
 
 
-def grid_kernel(mb_ref, ga_ref, tw_ref, out_ref, hs, xs, ts, rs, iota, *bufs):
+def grid_kernel(mb_ref, ga_ref, tw_ref, out_ref, hs, xs, ts, rs, *bufs):
     tabs, hots = bufs[:4], bufs[4:]
     mb = mb_ref[0]
-    iota[...] = lax.broadcasted_iota(jnp.int32, (256, 128), 0).astype(F32).astype(BF16)
+    sub = lax.broadcasted_iota(jnp.int32, (8, 128), 0).astype(F32)
 
     def fill(zh, band, g):
         start = g * 8 * 96 + zh * 48 + band
@@ -248,16 +248,12 @@
             for v in range(2):
                 a = xs[g, v, pl.ds(dev, 8, stride=8), :]
                 b = xs[g, 2 + v, pl.ds(dev, 8, stride=8), :]
-                for k in range(0, 16, 2):
-                    tab[v * 128 + k * 8 : v * 128 + k * 8 + 16, lanes] = jnp.concatenate([a, b], axis=0).astype(BF16)
-                    if k < 14:
-                        a = t * b - a
-                        b = t * a - b
-            r = jnp.broadcast_to(rs[g, dev : dev + 1, :], (16, 128)).astype(BF16)
-            for j in range(16):
-                hot[j * 16 : j * 16 + 16, lanes] = jnp.where(
-                    iota[j * 16 : j * 16 + 16] == r, jnp.ones((), BF16), jnp.zeros((), BF16)
-                )
+                for k in range(16):
+                    tab[v * 128 + k * 8 : v * 128 + k * 8 + 8, lanes] = a
+                    a, b = b, t * b - a
+            r = jnp.broadcast_to(rs[g, dev : dev + 1, :], (8, 128)) - sub
+            for j in range(32):
+                hot[j * 8 : j * 8 + 8, lanes] = jnp.where(r == 8.0 * j, 1.0, 0.0)
 
     def product(g):
         return lax.dot_general(tabs[g][...], hots[g][...], NT, preferred_element_type=F32)
@@ -307,9 +303,8 @@
             pltpu.VMEM((4, 4, 64, 128), F32),
             pltpu.VMEM((4, 8, 128), F32),
             pltpu.VMEM((4, 8, 128), F32),
-            pltpu.VMEM((256, 128), BF16),
         ]
-        + [pltpu.VMEM((256, 1024), BF16)] * 8,
+        + [pltpu.VMEM((256, 1024), F32)] * 8,
         compiler_params=pltpu.CompilerParams(vmem_limit_bytes=32 << 20),
         name="gridvis",
     )(mb, ga, tw)
@@ -405,7 +400,7 @@
     def put(i, half, value):
         out_ref[pl.ds(half * 512 + i, 32, stride=16), :] = value
 
-    lag1, lag2, lag3 = 1, 3, 5
+    lag1, lag2, lag3 = 4, 8, 12
 
     def turn(i, _):
         @pl.when(i < 16)
@@ -486,7 +481,7 @@
     ga, wo = exchange_call(s.reshape(2, 4, 16, 128), w)
     mb = lax.axis_index("tile") * 256 + (lax.axis_index("plane") // 4) * 128
     hp = grid_call(mb.astype(F32).reshape(1), ga.reshape(32 * 96, 128), jnp.asarray(tw))
-    ab = jnp.stack([taps, taps.astype(BF16).astype(F32)])
+    ab = jnp.stack([taps, lax.reduce_precision(taps, 8, 7)])
     halves = image_call(ab, hp, wo, jnp.asarray(dm))
     return jnp.concatenate([halves[:512], halves[512:]], axis=1)
 

time: 129 us -> 90.8 us (0.70)
  Pallas kernels: 124 us -> 86.1 us
    pallas_call x1, Pallas kernels: 50.7 us -> 28.6 us  [grid_call(): pl.pallas_call(grid_kernel, out_shape=jax.ShapeDtypeStruct((2, 16, 256, 2...]
    pallas_call x1, Pallas kernels: 46.4 us -> 30.7 us  [image_call(): pl.pallas_call(image_kernel, out_shape=jax.ShapeDtypeStruct((1024, 128),...]
where the time goes in v2:
time: 90.8 us; the launch traced here: 90.5 us
  Pallas kernels  86.1 us (95%)
  local copies, waits for them, and re-layouts  2.8 us (3%)
    pallas_call x1, Pallas kernels, image_call(): pl.pallas_call(image_kernel, out_shape=jax.ShapeDtypeStruct((1024, 128),...  30.7 us
    pallas_call x1, Pallas kernels, grid_call(): pl.pallas_call(grid_kernel, out_shape=jax.ShapeDtypeStruct((2, 16, 256, 2...  28.6 us
    pallas_call x1, Pallas kernels, exchange_call(): pl.pallas_call(exchange_kernel, out_shape=(jax.ShapeDtypeStruct((4, 4, 2,...  23.8 us
    pallas_call x1, Pallas kernels, sort_call(): pl.pallas_call(sort_kernel, out_shape=jax.ShapeDtypeStruct((128, 128), F3...  3.05 us
    unnamed x10, local copies, waits for them, and re-layouts  2.17 us

profile of v2, /device:TPU:0, one launch (start us, length us, event | category | flops | bytes accessed | tf_op | source)
XLA Modules:
  0.0 90.5 jit_solution(1869801323518531210)
XLA Ops:
  0.0 0.0 copy-start.4
  0.0 3.0 %sortvis.1 = f32[128,128]{1,0:T(8,128)} custom-call(f32[2,2048]{1,0:T(2,128)} %vis_ref.1, s32[1,2048]{1,0:T(1,128)} %bitcast.12, s32[1,2048]{1,0:T(1,128)} %bitcast.13), custom_call_target="tpu_custom_call" | custom-call | tf_op jit(solution)/shard_map/sortvis/pallas_call | solution.py:78
  3.7 0.6 broadcast_in_dim.8.w_ref
  4.3 23.8 %exchangevis.1 = (f32[4,4,2,2,3,16,128]{6,5,4,3,2,1,0:T(8,128)}, f32[2,8,128]{2,1,0:T(8,128)}) custom-call(f32[2,4,16,128]{3,2,1,0:T(8,128)} %bitcast.11, f32[8,128]{1,0:T(8,128)} %broadcast_in_dim.8.w_ref), custom_call_target="tpu_custom_call" | custom-call | tf_op jit(solution)/shard_map/exchangevis/pallas_call | solution.py:168
  28.1 0.0 copy-start
  28.1 1.4 %copy-done = f32[4,4,2,2,3,16,128]{6,5,4,3,2,1,0:T(8,128)S(1)} copy-done((f32[4,4,2,2,3,16,128]{6,5,4,3,2,1,0:T(8,128)S(1)}, f32[4,4,2,2,3,16,128]{6,5,4,3,2,1,0:T(8,128)}, u32[]{:S(2)}) %copy-start) | copy-done | bytes 1572888
  29.5 0.0 copy-start.2
  29.5 0.8 copy-done.2
  30.2 0.0 copy-start.1
  30.2 0.0 copy-start.3
  30.2 28.6 %gridvis.1.hp_ref = bf16[2,16,256,256]{3,2,1,0:T(8,128)(2,1)S(1)} custom-call(f32[1]{0:T(128)} %bitcast.2.mb_ref, f32[3072,128]{1,0:T(8,128)S(1)} %bitcast.10, f32[2,16,256]{2,1,0:T(8,128)S(1)} %copy-done.2), custom_call_target="tpu_custom_call" | custom-call | tf_op jit(solution)/shard_map/gridvis/pallas_call | solution.py:296
  58.9 0.0 copy-done.4
  58.9 0.0 copy-done.1
  58.9 0.0 copy-done.3
  58.9 30.7 %imagesum.1 = f32[1024,128]{1,0:T(8,128)S(1)} custom-call(f32[2,8]{1,0:T(2,128)S(1)} %pad_maximum_fusion.1.ab_ref, bf16[2,16,256,256]{3,2,1,0:T(8,128)(2,1)S(1)} %gridvis.1.hp_ref, f32[2,8,128]{2,1,0:T(8,128)S(1)} %copy-done.3, bf16[512,256]{1,0:T(8,128)(2,1)S(1)} %copy-done.1), custom_call_target="tpu_custom_call" | custom-call | tf_op jit(solution)/shard_map/imagesum/pallas_call | solution.py:454
  89.6 0.8 pad_maximum_fusion
  (3 shorter events, 0.0 us)
Async XLA Ops:
  0.0 58.9 %copy-start.4 = (f32[8]{0:T(128)S(1)}, f32[8]{0:T(128)}, u32[]{:S(2)}) copy-start(f32[8]{0:T(128)} %param.10) | copy-start | bytes 100
  28.1 1.4 %copy-start = (f32[4,4,2,2,3,16,128]{6,5,4,3,2,1,0:T(8,128)S(1)}, f32[4,4,2,2,3,16,128]{6,5,4,3,2,1,0:T(8,128)}, u32[]{:S(2)}) copy-start(f32[4,4,2,2,3,16,128]{6,5,4,3,2,1,0:T(8,128)} %get-tuple-element.7) | copy-start | bytes 4718596
  29.5 0.8 copy-start.2
  30.2 28.7 %copy-start.1 = (bf16[512,256]{1,0:T(8,128)(2,1)S(1)}, bf16[512,256]{1,0:T(8,128)(2,1)}, u32[]{:S(2)}) copy-start(bf16[512,256]{1,0:T(8,128)(2,1)} %constant.34.clone.dm_ref) | copy-start | bytes 786436
  30.2 28.7 %copy-start.3 = (f32[2,8,128]{2,1,0:T(8,128)S(1)}, f32[2,8,128]{2,1,0:T(8,128)}, u32[]{:S(2)}) copy-start(f32[2,8,128]{2,1,0:T(8,128)} %get-tuple-element.8.w_ref) | copy-start | bytes 24580

commit v3 on v2

v3 whole, which is shorter than its diff:
```python
import math

import jax
import jax.numpy as jnp
import numpy as np
from jax import lax
from jax.experimental import pallas as pl
from jax.experimental.pallas import tpu as pltpu
from jax.sharding import PartitionSpec as P


G = 4096
KS = 8
MESH = pl.DeviceIdType.MESH
F32 = jnp.float32
BF16 = jnp.bfloat16
NT = (((1,), (1,)), ((), ()))

SIN = (3.1415927410125732, -5.167710304260254, 2.550077438354492, -0.598291277885437, 0.07765766233205795)
COS = (0.9999999403953552, -4.934792995452881, 4.058411121368408, -1.331876516342163, 0.21968960762023926)


def poly(coefs, g):
    out = g * coefs[-1] + coefs[-2]
    for c in coefs[-3::-1]:
        out = out * g + c
    return out


def cos_sin(cycles):
    f = cycles - jnp.floor(cycles + 0.5)
    g = f * f
    s = f * poly(SIN, g)
    c = poly(COS, g)
    s2 = s + s
    return 1.0 - s2 * s, s2 * c


def rotated(re, im, c, s):
    return re * c - im * s, re * s + im * c


def dft(re, im):
    n = len(re)
    if n == 1:
        return re, im
    er, ei = dft(re[0::2], im[0::2])
    dr, di = dft(re[1::2], im[1::2])
    h = n // 2
    out_r, out_i = [None] * n, [None] * n
    for k in range(h):
        if k == 0:
            tr, ti = dr[k], di[k]
        elif 4 * k == n:
            tr, ti = -di[k], dr[k]
        elif 8 * k == n:
            q = math.sqrt(0.5)
            tr, ti = (dr[k] - di[k]) * q, (dr[k] + di[k]) * q
        elif 8 * k == 3 * n:
            q = math.sqrt(0.5)
            tr, ti = (dr[k] + di[k]) * -q, (dr[k] - di[k]) * q
        else:
            c, s = math.cos(2 * math.pi * k / n), math.sin(2 * math.pi * k / n)
            tr, ti = dr[k] * c - di[k] * s, dr[k] * s + di[k] * c
        out_r[k], out_i[k] = er[k] + tr, ei[k] + ti
        out_r[k + h], out_i[k + h] = er[k] - tr, ei[k] - ti
    return out_r, out_i


def sort(vis_ref, tgt_ref, off_ref, out_ref):
    count = tgt_ref.shape[1]
    blk = 256
    ii = lax.broadcasted_iota(jnp.int32, (blk, blk), 0)
    jj = lax.broadcasted_iota(jnp.int32, (blk, blk), 1)
    tri = jnp.where(ii < jj, 1.0, 0.0).astype(BF16)
    rows = lax.broadcasted_iota(jnp.int32, (128, blk), 0)
    ranks = lax.broadcasted_iota(jnp.int32, (32, blk), 0).astype(F32)
    carry = jnp.zeros((128, 1), F32)
    acc = jnp.zeros((128, 128), F32)
    for b in range(count // blk):
        sl = slice(b * blk, (b + 1) * blk)
        one = jnp.where(rows == tgt_ref[:, sl], 1.0, 0.0)
        oneb = one.astype(BF16)
        before = jnp.dot(oneb, tri, preferred_element_type=F32)
        rank = jnp.sum(one * (before + carry), axis=0, keepdims=True)
        carry = carry + jnp.sum(one, axis=1, keepdims=True)
        hit = ranks == rank
        off = off_ref[:, sl]
        parts = [((off >> 12) << 12).astype(F32), (((off >> 4) & 255) << 4).astype(F32), (off & 15).astype(F32)]
        left = [vis_ref[0:1, sl], vis_ref[1:2, sl]]
        for k in range(3):
            cols = []
            for v in range(2):
                top = left[v].astype(BF16).astype(F32)
                left[v] = left[v] - top
                cols.append(jnp.where(hit, top, 0.0))
            cols.append(jnp.where(hit, parts[k], 0.0))
            cols.append(jnp.zeros((32, blk), F32))
            table = jnp.concatenate(cols, axis=0).astype(BF16)
            acc = acc + lax.dot_general(oneb, table, NT, preferred_element_type=F32)
    for q in range(8):
        out_ref[q // 4, q % 4] = acc[q * 16 : q * 16 + 16]


def place():
    p = lax.axis_index("plane")
    t = lax.axis_index("tile")
    return p // 4, p % 4, t // 8, (t // 2) % 4, t % 2


def kernel(w_ref, ab_ref, vis_ref, tgt_ref, off_ref, tw_ref, dm_ref, out_ref, *scratch):
    sb, wb, wo, ra, ga, hs, hp, xs, ts, rs, sr, si, pb, r1, fw, rc, rd, zb, zr = scratch[:19]
    sa, qa, sy, qy, sv, qv, sc, qc, sw, qw, s1, q1, sf, qf, sd, qd, sz, qz = scratch[19:]
    zh, x, zl, y, core = place()
    z = zh * 2 + zl
    p, t = zh * 4 + x, zl * 8 + y * 2 + core
    xp, xm = (x + 1) % 4, (x + 3) % 4

    def at_x(d):
        return {"plane": zh * 4 + (x + d) % 4, "tile": t}

    def at_y(d):
        return {"plane": p, "tile": zl * 8 + ((y + d) % 4) * 2 + core}

    def at_z(d):
        zz = (z + d) % 4
        return {"plane": (zz // 2) * 4 + x, "tile": (zz % 2) * 8 + y * 2 + core}

    partner = {"plane": p, "tile": zl * 8 + y * 2 + (1 - core)}
    right, left, across = at_x(1), at_x(3), at_z(2)

    barrier = pltpu.get_barrier_semaphore()
    for d in (1, 2, 3):
        for at in (at_x, at_y, at_z):
            pl.semaphore_signal(barrier, inc=1, device_id=at(d), device_id_type=MESH)
    pl.semaphore_signal(barrier, inc=1, device_id=partner, device_id_type=MESH)

    def copy(src, dst, send, recv, device):
        return pltpu.make_async_remote_copy(
            src_ref=src, dst_ref=dst, send_sem=send, recv_sem=recv, device_id=device, device_id_type=MESH
        )

    sort(vis_ref, tgt_ref, off_ref, sb)
    wb[...] = jnp.full((8, 128), w_ref[0])
    wo[zh] = wb[...]
    pl.semaphore_wait(barrier, 10)
    first = [copy(sb.at[:, (x + d) % 4], ra.at[x], sa.at[d - 1], qa.at[d - 1], at_x(d)) for d in (1, 2, 3)]
    for c in first:
        c.start()
    ra[x] = sb[:, x]

    l0 = lax.broadcasted_iota(jnp.int32, (256, 128), 0)
    lane = lax.broadcasted_iota(jnp.int32, (256, 128), 1)
    ec, es = cos_sin((l0 * 16 + lane).astype(F32) * (1.0 / G))
    ar, ai = jnp.full((256, 128), ab_ref[0, KS - 1]), jnp.zeros((256, 128), F32)
    for j in range(KS - 2, -1, -1):
        ar, ai = rotated(ar, ai, ec, es)
        ar = ar + ab_ref[0, j]
    sr[...] = ar
    si[...] = ai

    for c in first:
        c.wait()

    def rows_of(zrow, cr):
        return ga.at[pl.ds(pl.multiple_of((zrow * 2 + cr) * 384, 384), 384)]

    got = [ra[s].reshape(32, 128) for s in range(4)]
    group = lax.broadcasted_iota(jnp.int32, (32, 128), 1) // 32
    base = pl.multiple_of(((z * 2 + core) * 4 + y) * 96, 96)
    for k in range(3):
        row = jnp.zeros((32, 128), F32)
        for s in range(4):
            shift = (32 * (s - k)) % 128
            moved = pltpu.roll(got[s], shift, 1) if shift else got[s]
            row = jnp.where(group == s, moved, row)
        ga[pl.ds(base + k * 16, 16)] = row[:16]
        ga[pl.ds(base + 48 + k * 16, 16)] = row[16:]
    mine = ga.at[pl.ds(base, 96)]
    ring = [copy(mine, mine, sy.at[d - 1], qy.at[d - 1], at_y(d)) for d in (1, 3, 2)]
    for c in ring:
        c.start()
    wcopy = copy(wb, wo.at[zh], sw, qw, across)
    wcopy.start()

    def clear(i, _):
        hs[i // 16, i % 16] = jnp.zeros((256, 256), F32)
        return 0

    lax.fori_loop(0, 32, clear, 0)
    for c in ring:
        c.wait()

    def zrow_of(g):
        return (z + jnp.where(g == 0, 0, jnp.where(g == 1, 3, g - 1))) % 4

    own = rows_of(z, core)
    rings = [copy(own, own, sv.at[g], qv.at[g], at_z(d)) for g, d in ((0, 1), (1, 3), (2, 2))]

    def arrival(g):
        part = rows_of(zrow_of(g), core)
        return copy(part, part, sv.at[g - 1], qv.at[g - 1], across)

    def swap(g):
        part = rows_of(zrow_of(g), core)
        return copy(part, part, sc.at[g], qc.at[g], partner)

    def swapped(g):
        part = rows_of(zrow_of(g), 1 - core)
        return copy(part, part, sc.at[g], qc.at[g], partner)

    swap(0).start()
    for c in rings:
        c.start()

    mb = (t * 256 + zh * 128).astype(F32)
    sub = lax.broadcasted_iota(jnp.int32, (8, 128), 0).astype(F32)

    def dense(start, u):
        re = ga[pl.ds(start, 8, stride=96), :]
        im = ga[pl.ds(start + 16, 8, stride=96), :]
        off = ga[pl.ds(start + 32, 8, stride=96), :]
        row = jnp.floor(off * (1.0 / G))
        col = off - row * G
        cb, sb_ = cos_sin(col * mb * (1.0 / G))
        c1, s1_ = cos_sin(col * (1.0 / G))
        c8, s8 = cos_sin(col * (8.0 / G))
        re, im = rotated(re, im, cb, sb_)
        for s in range(8):
            nr, ni = rotated(re, im, c8, s8)
            xs[u, 0, s * 8 : s * 8 + 8] = re
            xs[u, 1, s * 8 : s * 8 + 8] = im
            xs[u, 2, s * 8 : s * 8 + 8] = nr
            xs[u, 3, s * 8 : s * 8 + 8] = ni
            if s < 7:
                re, im = rotated(re, im, c1, s1_)
        ts[u] = c8 + c8
        rs[u] = row

    def product(u):
        tabs, hots = [], []
        for dev in range(8):
            turn = jnp.broadcast_to(ts[u, dev : dev + 1, :], (8, 128))
            rows = []
            for v in range(2):
                a = xs[u, v, pl.ds(dev, 8, stride=8), :]
                b = xs[u, 2 + v, pl.ds(dev, 8, stride=8), :]
                for k in range(16):
                    rows.append(a)
                    a, b = b, turn * b - a
            tabs.append(jnp.concatenate(rows, axis=0))
            r = jnp.broadcast_to(rs[u, dev : dev + 1, :], (8, 128)) - sub
            r = jnp.concatenate([r, r - 8.0], axis=0).astype(BF16)
            one, zero = jnp.ones((), BF16), jnp.zeros((), BF16)
            hots.append(
                jnp.concatenate([jnp.where(r == jnp.asarray(16.0 * j, BF16), one, zero) for j in range(16)], axis=0)
            )
        tab, hot = jnp.concatenate(tabs, axis=1), jnp.concatenate(hots, axis=1)
        return lax.dot_general(tab, hot, NT, preferred_element_type=F32)

    def segment(n, _):
        g, half = n // 2, n % 2

        @pl.when(jnp.logical_and(half == 1, g < 3))
        def _():
            arrival(g + 1).wait_recv()
            swap(g + 1).start()

        @pl.when(half == 0)
        def _():
            swapped(g).wait_recv()

        start = zrow_of(g) * 768 + half * 48
        for u in range(4):
            dense(start + u, u)

        def quad(it, _):
            for u in range(4):
                hs[half, it * 4 + u] += product(u)
            following = start + jnp.minimum(it + 1, 3) * 4
            for u in range(4):
                dense(following + u, u)
            return 0

        lax.fori_loop(0, 4, quad, 0)
        return 0

    lax.fori_loop(0, 8, segment, 0)

    def strip(i, _):
        v = i // 8
        m = pl.multiple_of(i % 8 * 16, 16)
        for h in range(2):
            lanes = slice(h * 128, h * 128 + 128)
            re = [hs[v, b, pl.ds(m, 16), lanes] for b in range(16)]
            im = [hs[v, b, pl.ds(m + 128, 16), lanes] for b in range(16)]
            re, im = dft(re, im)
            for q in range(16):
                a, b = re[q], im[q]
                if q:
                    a, b = rotated(a, b, tw_ref[0, q : q + 1, lanes], tw_ref[1, q : q + 1, lanes])
                hp[v, q, pl.ds(m, 16), lanes] = a.astype(BF16)
                hp[v, q, pl.ds(m + 128, 16), lanes] = b.astype(BF16)
        return 0

    lax.fori_loop(0, 16, strip, 0)
    wcopy.wait()

    m = t * 256 + zh * 128 + lax.broadcasted_iota(jnp.int32, (8, 128), 1)
    ec, es = cos_sin(m.astype(F32) * (1.0 / G))
    tr, ti = jnp.full((8, 128), ab_ref[1, KS - 1]), jnp.zeros((8, 128), F32)
    for j in range(KS - 2, -1, -1):
        tr, ti = rotated(tr, ti, ec, es)
        tr = tr + ab_ref[1, j]
    tr, ti = tr[0:1] * (1.0 / 512.0), ti[0:1] * (1.0 / 512.0)
    ym = jnp.where(m >= G // 2, m - G, m).astype(F32)[0:1] * (0.5 / G)
    ysq = ym * ym
    ws = [wo[q, 0:1, :] for q in range(2)]
    row64 = lax.broadcasted_iota(jnp.int32, (64, 128), 0)
    lane64 = lax.broadcasted_iota(jnp.int32, (64, 128), 1)

    def step_one(i):
        xo = (x + 2) % 4
        return (
            copy(pb.at[i, 0, xo], r1.at[i, 0], s1.at[i, 0], q1.at[i, 0], right),
            copy(pb.at[i, 1, xo], r1.at[i, 1], s1.at[i, 1], q1.at[i, 1], left),
        )

    def direct(i):
        return (
            copy(pb.at[i, 0, xm], rd.at[i, 0], sd.at[i, 0], qd.at[i, 0], left),
            copy(pb.at[i, 1, xp], rd.at[i, 1], sd.at[i, 1], qd.at[i, 1], right),
        )

    def forward(i):
        return (
            copy(fw.at[i, 0], rc.at[i, 0], sf.at[i, 0], qf.at[i, 0], right),
            copy(fw.at[i, 1], rc.at[i, 1], sf.at[i, 1], qf.at[i, 1], left),
        )

    def over(i):
        return copy(zb.at[i], zr.at[i], sz.at[i], qz.at[i], across)

    def compute(i):
        for q in range(4):
            rows = slice(q * 64, q * 64 + 64)
            l = (row64 + q * 64) * 16 + i
            xl = jnp.where(l >= G // 2, l - G, l).astype(F32) * (0.5 / G)
            rho = xl * xl + ysq
            n = -rho / (1.0 + jnp.sqrt(1.0 - rho))
            zre = zim = None
            for v in range(2):
                h = hp[v, i]
                pc = lax.dot_general(dm_ref[rows, :], h, NT, preferred_element_type=F32)
                ps = lax.dot_general(dm_ref[256 + q * 64 : 320 + q * 64, :], h, NT, preferred_element_type=F32)
                dre = pc[:, :128] - ps[:, 128:]
                dim = ps[:, :128] + pc[:, 128:]
                c, s = cos_sin(ws[v] * n)
                a, b = rotated(dre, dim, c, s)
                zre, zim = (a, b) if zre is None else (zre + a, zim + b)
            a, b = rotated(zre, zim, tr, ti)
            cs = jnp.sum(jnp.where(lane64 == i, sr[rows], 0.0), axis=1, keepdims=True)
            ss = jnp.sum(jnp.where(lane64 == i, si[rows], 0.0), axis=1, keepdims=True)
            part = cs * a - ss * b
            for k in range(2):
                pb[i, q // 2, (q % 2) * 2 + k] = part[k * 32 : k * 32 + 32]

    def put(i, half, value):
        out_ref[pl.ds(half * 512 + i, 32, stride=16), :] = value

    lag1, lag2, lag3 = 4, 8, 12

    def turn(i, _):
        @pl.when(i < 16)
        def _():
            compute(i)
            for c in step_one(i) + direct(i):
                c.start()

        @pl.when(jnp.logical_and(i >= lag1, i < 16 + lag1))
        def _():
            j = i - lag1
            for c in step_one(j):
                c.wait_recv()
            fw[j, 0] = r1[j, 0] + pb[j, 0, xp]
            fw[j, 1] = r1[j, 1] + pb[j, 1, xm]
            for c in forward(j):
                c.start()

        @pl.when(jnp.logical_and(i >= lag2, i < 16 + lag2))
        def _():
            j = i - lag2
            for c in forward(j) + direct(j):
                c.wait_recv()
            put(j, zh, pb[j, zh, x] + rc[j, zh] + rd[j, zh])
            zb[j] = pb[j, 1 - zh, x] + rc[j, 1 - zh] + rd[j, 1 - zh]
            over(j).start()

        @pl.when(i >= lag3)
        def _():
            j = i - lag3
            over(j).wait_recv()
            put(j, 1 - zh, zr[j])

        return 0

    lax.fori_loop(0, 16 + lag3, turn, 0)

    def drain(i, _):
        for c in step_one(i) + direct(i) + forward(i) + (over(i),):
            c.wait_send()
        return 0

    lax.fori_loop(0, 16, drain, 0)
    for c in rings:
        c.wait_send()
    for g in range(4):
        swap(g).wait_send()

def constants():
    k = np.arange(256)
    a = 2 * np.pi * (np.outer(k, k) % 256) / 256
    dm = np.concatenate([np.cos(a), np.sin(a)], axis=0)
    b = 2 * np.pi * np.outer(np.arange(16), k) / G
    return dm.astype(jnp.bfloat16), np.stack([np.cos(b), np.sin(b)]).astype(np.float32)

def local(visibility, target, offset, taps, w_plane):
    dm, tw = constants()
    count = visibility.shape[1]
    ab = jnp.stack([taps, lax.reduce_precision(taps, 8, 7)])
    dma = pltpu.SemaphoreType.DMA
    vmem = pl.BlockSpec(memory_space=pltpu.VMEM)
    smem = pl.BlockSpec(memory_space=pltpu.SMEM)
    buf = pltpu.VMEM((16, 2, 32, 128), F32)
    part = pltpu.VMEM((16, 32, 128), F32)
    halves = pl.pallas_call(
        kernel,
        out_shape=jax.ShapeDtypeStruct((1024, 128), F32),
        in_specs=[smem, smem] + [vmem] * 5,
        out_specs=vmem,
        scratch_shapes=[
            pltpu.VMEM((2, 4, 16, 128), F32),
            pltpu.VMEM((8, 128), F32),
            pltpu.VMEM((2, 8, 128), F32),
            pltpu.VMEM((4, 2, 16, 128), F32),
            pltpu.VMEM((3072, 128), F32),
            pltpu.VMEM((2, 16, 256, 256), F32),
            pltpu.VMEM((2, 16, 256, 256), BF16),
            pltpu.VMEM((4, 4, 64, 128), F32),
            pltpu.VMEM((4, 8, 128), F32),
            pltpu.VMEM((4, 8, 128), F32),
            pltpu.VMEM((256, 128), F32),
            pltpu.VMEM((256, 128), F32),
            pltpu.VMEM((16, 2, 4, 32, 128), F32),
            buf,
            buf,
            buf,
            buf,
            part,
            part,
        ]
        + [dma((3,))] * 6
        + [dma((4,))] * 2
        + [dma] * 2
        + [dma((16, 2))] * 6
        + [dma((16,))] * 2,
        compiler_params=pltpu.CompilerParams(collective_id=0, has_side_effects=True, vmem_limit_bytes=56 << 20),
        name="dirtyimage",
    )(w_plane, ab, visibility, target.reshape(1, count), offset.reshape(1, count), jnp.asarray(tw), jnp.asarray(dm))
    return jnp.concatenate([halves[:512], halves[512:]], axis=1)


def solution(mesh):
    both = ("plane", "tile")
    return jax.shard_map(
        local,
        mesh=mesh,
        in_specs=(P(None, both), P(both, None), P(both), P(), P("plane")),
        out_specs=P("plane", "tile"),
        check_vma=False,
    )
```

time: 90.8 us -> 87.8 us (0.967)
  Pallas kernels: 86.1 us -> 83.8 us
  local copies, waits for them, and re-layouts: 2.8 us -> 1.71 us
    pallas_call x4 -> x1, Pallas kernels: 86.1 us -> 83.8 us  [local(): pl.pallas_call(kernel, out_shape=jax.ShapeDtypeStruct((1024, 128), F32),...]
    unnamed x10 -> x2, local copies, waits for them, and re-layouts: 2.17 us -> 0.65 us
    slice x1, local copies, waits for them, and re-layouts: 0.04 us -> 1.07 us  [local(): return jnp.concatenate([halves[:512], halves[512:]], axis=1)]
where the time goes in v3:
time: 87.8 us; the launch traced here: 87.6 us
  Pallas kernels  83.8 us (95%)
  local copies, waits for them, and re-layouts  1.71 us (2%)
  other arithmetic  1.4 us (2%)
    pallas_call x1, Pallas kernels, local(): pl.pallas_call(kernel, out_shape=jax.ShapeDtypeStruct((1024, 128), F32),...  83.8 us

profile of v3, /device:TPU:0, one launch (start us, length us, event | category | flops | bytes accessed | tf_op | source)
XLA Modules:
  0.0 87.6 jit_solution(947950771117699750)
XLA Ops:
  0.7 0.0 copy-start
  0.7 0.6 copy-done
  1.3 0.6 pad_maximum_fusion.1.ab_ref
  1.9 83.8 %dirtyimage.1 = f32[1024,128]{1,0:T(8,128)} custom-call(f32[1]{0:T(128)S(6)} %copy.8.w_ref, f32[2,8]{1,0:T(2,128)} %pad_maximum_fusion.1.ab_ref, f32[2,2048]{1,0:T(2,128)} %vis_ref.1, s32[1,2048]{1,0:T(1,128)} %bitcast.5, s32[1,2048]{1,0:T(1,128)} %bitcast.6, f32[2,16,256]{2,1,0:T(8,128)} %constant.4.clone.tw_ref, bf16[512,256]{1,0:T(8,128)(2,1)} %constant.5.clone.dm_ref), custom_call_target="tpu_custom_call" | custom-call | tf_op jit(solution)/shard_map/dirtyimage/pallas_call | solution.py:436
  85.7 1.1 %fusion = (f32[512,128]{1,0:T(8,128)S(1)}, f32[512,128]{1,0:T(8,128)S(1)}) fusion(f32[1024,128]{1,0:T(8,128)} %dirtyimage.1), kind=kLoop, calls=%fused_computation.3 | loop fusion | bytes 1048576 | tf_op jit(solution)/shard_map/slice | solution.py:470
  86.8 0.8 pad_maximum_fusion
  (1 shorter events, 0.0 us)
Async XLA Ops:
  0.7 0.7 copy-start

commit v4 on v3

--- a/solution.py
+++ b/solution.py
@@ -2,7 +2,6 @@
 
 import jax
 import jax.numpy as jnp
-import numpy as np
 from jax import lax
 from jax.experimental import pallas as pl
 from jax.experimental.pallas import tpu as pltpu
@@ -108,9 +107,9 @@
     return p // 4, p % 4, t // 8, (t // 2) % 4, t % 2
 
 
-def kernel(w_ref, ab_ref, vis_ref, tgt_ref, off_ref, tw_ref, dm_ref, out_ref, *scratch):
-    sb, wb, wo, ra, ga, hs, hp, xs, ts, rs, sr, si, pb, r1, fw, rc, rd, zb, zr = scratch[:19]
-    sa, qa, sy, qy, sv, qv, sc, qc, sw, qw, s1, q1, sf, qf, sd, qd, sz, qz = scratch[19:]
+def kernel(w_ref, taps_ref, vis_ref, tgt_ref, off_ref, out_ref, *scratch):
+    sb, wb, wo, ra, ga, hs, hp, eq, dm, tw, xs, ts, rs, sr, si, pb, r1, fw, rc, rd, zb, zr = scratch[:22]
+    sa, qa, sn, qn, sv, qv, sc, qc, sw, qw, s1, q1, sf, qf, sd, qd, sz, qz = scratch[22:]
     zh, x, zl, y, core = place()
     z = zh * 2 + zl
     p, t = zh * 4 + x, zl * 8 + y * 2 + core
@@ -144,82 +143,135 @@
     wb[...] = jnp.full((8, 128), w_ref[0])
     wo[zh] = wb[...]
     pl.semaphore_wait(barrier, 10)
-    first = [copy(sb.at[:, (x + d) % 4], ra.at[x], sa.at[d - 1], qa.at[d - 1], at_x(d)) for d in (1, 2, 3)]
+    first = [copy(sb.at[:, (x + d) % 4], ra.at[x], sa.at[d - 1], qa.at[d - 1], at_x(d)) for d in (1, 3, 2)]
     for c in first:
         c.start()
+    wcopy = copy(wb, wo.at[zh], sw, qw, across)
+    wcopy.start()
     ra[x] = sb[:, x]
 
     l0 = lax.broadcasted_iota(jnp.int32, (256, 128), 0)
     lane = lax.broadcasted_iota(jnp.int32, (256, 128), 1)
     ec, es = cos_sin((l0 * 16 + lane).astype(F32) * (1.0 / G))
-    ar, ai = jnp.full((256, 128), ab_ref[0, KS - 1]), jnp.zeros((256, 128), F32)
+    ar, ai = jnp.full((256, 128), taps_ref[KS - 1]), jnp.zeros((256, 128), F32)
     for j in range(KS - 2, -1, -1):
         ar, ai = rotated(ar, ai, ec, es)
-        ar = ar + ab_ref[0, j]
+        ar = ar + taps_ref[j]
     sr[...] = ar
     si[...] = ai
-
+    m = t * 256 + zh * 128 + lax.broadcasted_iota(jnp.int32, (8, 128), 1)
+    ec, es = cos_sin(m.astype(F32) * (1.0 / G))
+    taps_low = [jnp.full((8, 128), taps_ref[j]).astype(BF16).astype(F32) for j in range(KS)]
+    tr, ti = taps_low[KS - 1], jnp.zeros((8, 128), F32)
+    for j in range(KS - 2, -1, -1):
+        tr, ti = rotated(tr, ti, ec, es)
+        tr = tr + taps_low[j]
+    tr, ti = tr[0:1] * (1.0 / 512.0), ti[0:1] * (1.0 / 512.0)
+    ym = jnp.where(m >= G // 2, m - G, m).astype(F32)[0:1] * (0.5 / G)
+    ysq = ym * ym
+    row64 = lax.broadcasted_iota(jnp.int32, (64, 128), 0)
+    lane64 = lax.broadcasted_iota(jnp.int32, (64, 128), 1)
+
+    def screen(n, _):
+        v = jnp.where(n < 16, zh, 1 - zh)
+        i = n % 16
+        w = wo[v, 0:1, :]
+        for q in range(4):
+            rows = slice(q * 64, q * 64 + 64)
+            l = (row64 + q * 64) * 16 + i
+            xl = jnp.where(l >= G // 2, l - G, l).astype(F32) * (0.5 / G)
+            rho = xl * xl + ysq
+            n_minus = -rho / (1.0 + jnp.sqrt(1.0 - rho))
+            c, s = cos_sin(w * n_minus)
+            c, s = rotated(c, s, tr, ti)
+            cs = jnp.sum(jnp.where(lane64 == i, sr[rows], 0.0), axis=1, keepdims=True)
+            ss = jnp.sum(jnp.where(lane64 == i, si[rows], 0.0), axis=1, keepdims=True)
+            c, s = rotated(c, s, cs, ss)
+            eq[v, i, 0, rows] = c
+            eq[v, i, 1, rows] = s
+        return 0
+
+    lax.fori_loop(0, 12, screen, 0)
     for c in first:
         c.wait()
 
-    def rows_of(zrow, cr):
-        return ga.at[pl.ds(pl.multiple_of((zrow * 2 + cr) * 384, 384), 384)]
+    outer, inner = (z, y), (y, z)
+    around = ((at_y, at_z), (at_z, at_y))
+
+    def rows_of(h, g, cr):
+        step = jnp.where(g == 0, 0, jnp.where(g == 1, 3, g - 1))
+        o = (outer[h] + step) % 4
+        return ga.at[pl.ds(pl.multiple_of(h * 1536 + (o * 2 + cr) * 192, 192), 192)]
 
     got = [ra[s].reshape(32, 128) for s in range(4)]
     group = lax.broadcasted_iota(jnp.int32, (32, 128), 1) // 32
-    base = pl.multiple_of(((z * 2 + core) * 4 + y) * 96, 96)
+    base = [pl.multiple_of(h * 1536 + ((outer[h] * 2 + core) * 4 + inner[h]) * 48, 48) for h in range(2)]
     for k in range(3):
         row = jnp.zeros((32, 128), F32)
         for s in range(4):
             shift = (32 * (s - k)) % 128
             moved = pltpu.roll(got[s], shift, 1) if shift else got[s]
             row = jnp.where(group == s, moved, row)
-        ga[pl.ds(base + k * 16, 16)] = row[:16]
-        ga[pl.ds(base + 48 + k * 16, 16)] = row[16:]
-    mine = ga.at[pl.ds(base, 96)]
-    ring = [copy(mine, mine, sy.at[d - 1], qy.at[d - 1], at_y(d)) for d in (1, 3, 2)]
-    for c in ring:
+        for h in range(2):
+            ga[pl.ds(base[h] + k * 16, 16)] = row[h * 16 : h * 16 + 16]
+    near = []
+    for d in (1, 3, 2):
+        for h in range(2):
+            mine = ga.at[pl.ds(base[h], 48)]
+            near.append(copy(mine, mine, sn.at[h, d - 1], qn.at[h, d - 1], around[h][0](d)))
+    for c in near:
         c.start()
-    wcopy = copy(wb, wo.at[zh], sw, qw, across)
-    wcopy.start()
-
-    def clear(i, _):
-        hs[i // 16, i % 16] = jnp.zeros((256, 256), F32)
-        return 0
-
-    lax.fori_loop(0, 32, clear, 0)
-    for c in ring:
+    wcopy.wait()
+    lax.fori_loop(12, 24, screen, 0)
+    for q in range(8):
+        a = lax.broadcasted_iota(jnp.int32, (32, 256), 0) + q * 32
+        b = lax.broadcasted_iota(jnp.int32, (32, 256), 1)
+        c, s = cos_sin(((a * b) % 256).astype(F32) * (1.0 / 256.0))
+        dm[q * 32 : q * 32 + 32] = c.astype(BF16)
+        dm[256 + q * 32 : 288 + q * 32] = s.astype(BF16)
+    a = lax.broadcasted_iota(jnp.int32, (16, 256), 0)
+    b = lax.broadcasted_iota(jnp.int32, (16, 256), 1)
+    c, s = cos_sin((a * b).astype(F32) * (1.0 / G))
+    tw[0] = c
+    tw[1] = s
+    for c in near:
         c.wait()
 
-    def zrow_of(g):
-        return (z + jnp.where(g == 0, 0, jnp.where(g == 1, 3, g - 1))) % 4
-
-    own = rows_of(z, core)
-    rings = [copy(own, own, sv.at[g], qv.at[g], at_z(d)) for g, d in ((0, 1), (1, 3), (2, 2))]
-
-    def arrival(g):
-        part = rows_of(zrow_of(g), core)
-        return copy(part, part, sv.at[g - 1], qv.at[g - 1], across)
-
-    def swap(g):
-        part = rows_of(zrow_of(g), core)
-        return copy(part, part, sc.at[g], qc.at[g], partner)
-
-    def swapped(g):
-        part = rows_of(zrow_of(g), 1 - core)
-        return copy(part, part, sc.at[g], qc.at[g], partner)
-
-    swap(0).start()
-    for c in rings:
+    far = []
+    for g, d in ((1, 1), (2, 3), (3, 2)):
+        for h in range(2):
+            own = rows_of(h, 0, core)
+            far.append(copy(own, own, sv.at[h, g], qv.at[h, g], around[h][1](d)))
+
+    def arrival(h, g):
+        part = rows_of(h, g, core)
+        return copy(part, part, sv.at[h, g], qv.at[h, g], across)
+
+    def swap(h, g):
+        part = rows_of(h, g, core)
+        return copy(part, part, sc.at[h, g], qc.at[h, g], partner)
+
+    def swapped(h, g):
+        part = rows_of(h, g, 1 - core)
+        return copy(part, part, sc.at[h, g], qc.at[h, g], partner)
+
+    for h in range(2):
+        swap(h, 0).start()
+    for c in far:
         c.start()
 
     mb = (t * 256 + zh * 128).astype(F32)
     sub = lax.broadcasted_iota(jnp.int32, (8, 128), 0).astype(F32)
 
+    def start_of(h, g):
+        step = jnp.where(g == 0, 0, jnp.where(g == 1, 3, g - 1))
+        o = (jnp.where(h == 0, outer[0], outer[1]) + step) % 4
+        return h * 1536 + o * 384
+
     def dense(start, u):
-        re = ga[pl.ds(start, 8, stride=96), :]
-        im = ga[pl.ds(start + 16, 8, stride=96), :]
-        off = ga[pl.ds(start + 32, 8, stride=96), :]
+        re = ga[pl.ds(start, 8, stride=48), :]
+        im = ga[pl.ds(start + 16, 8, stride=48), :]
+        off = ga[pl.ds(start + 32, 8, stride=48), :]
         row = jnp.floor(off * (1.0 / G))
         col = off - row * G
         cb, sb_ = cos_sin(col * mb * (1.0 / G))
@@ -250,42 +302,62 @@
                     a, b = b, turn * b - a
             tabs.append(jnp.concatenate(rows, axis=0))
             r = jnp.broadcast_to(rs[u, dev : dev + 1, :], (8, 128)) - sub
-            r = jnp.concatenate([r, r - 8.0], axis=0).astype(BF16)
-            one, zero = jnp.ones((), BF16), jnp.zeros((), BF16)
-            hots.append(
-                jnp.concatenate([jnp.where(r == jnp.asarray(16.0 * j, BF16), one, zero) for j in range(16)], axis=0)
-            )
+            hots.append(jnp.concatenate([jnp.where(r == 8.0 * j, 1.0, 0.0) for j in range(32)], axis=0))
+        return tabs, hots
+
+    def total(us):
+        tabs, hots = [], []
+        for u in us:
+            a, b = product(u)
+            tabs += a
+            hots += b
         tab, hot = jnp.concatenate(tabs, axis=1), jnp.concatenate(hots, axis=1)
         return lax.dot_general(tab, hot, NT, preferred_element_type=F32)
 
-    def segment(n, _):
-        g, half = n // 2, n % 2
-
-        @pl.when(jnp.logical_and(half == 1, g < 3))
-        def _():
-            arrival(g + 1).wait_recv()
-            swap(g + 1).start()
-
-        @pl.when(half == 0)
-        def _():
-            swapped(g).wait_recv()
-
-        start = zrow_of(g) * 768 + half * 48
-        for u in range(4):
-            dense(start + u, u)
+    def early(h, _):
+        start = start_of(h, 0)
 
         def quad(it, _):
             for u in range(4):
-                hs[half, it * 4 + u] += product(u)
-            following = start + jnp.minimum(it + 1, 3) * 4
+                dense(start + it * 4 + u, u)
             for u in range(4):
-                dense(following + u, u)
+                hs[h, it * 4 + u] = total([u])
             return 0
 
         lax.fori_loop(0, 4, quad, 0)
         return 0
 
-    lax.fori_loop(0, 8, segment, 0)
+    for h in range(2):
+        swapped(h, 0).wait_recv()
+    lax.fori_loop(0, 2, early, 0)
+    for g in (1, 2):
+        for h in range(2):
+            arrival(h, g).wait_recv()
+            swap(h, g).start()
+    lax.fori_loop(24, 32, screen, 0)
+    for h in range(2):
+        arrival(h, 3).wait_recv()
+        swap(h, 3).start()
+    for g in (1, 2, 3):
+        for h in range(2):
+            swapped(h, g).wait_recv()
+
+    def late(h, _):
+        starts = [start_of(h, g) for g in (1, 2, 3)]
+        for u in range(3):
+            dense(starts[u], u)
+
+        def one(band, _):
+            hs[h, band] += total([0, 1, 2])
+            following = jnp.minimum(band + 1, 15)
+            for u in range(3):
+                dense(starts[u] + following, u)
+            return 0
+
+        lax.fori_loop(0, 16, one, 0)
+        return 0
+
+    lax.fori_loop(0, 2, late, 0)
 
     def strip(i, _):
         v = i // 8
@@ -298,27 +370,12 @@
             for q in range(16):
                 a, b = re[q], im[q]
                 if q:
-                    a, b = rotated(a, b, tw_ref[0, q : q + 1, lanes], tw_ref[1, q : q + 1, lanes])
+                    a, b = rotated(a, b, tw[0, q : q + 1, lanes], tw[1, q : q + 1, lanes])
                 hp[v, q, pl.ds(m, 16), lanes] = a.astype(BF16)
                 hp[v, q, pl.ds(m + 128, 16), lanes] = b.astype(BF16)
         return 0
 
     lax.fori_loop(0, 16, strip, 0)
-    wcopy.wait()
-
-    m = t * 256 + zh * 128 + lax.broadcasted_iota(jnp.int32, (8, 128), 1)
-    ec, es = cos_sin(m.astype(F32) * (1.0 / G))
-    tr, ti = jnp.full((8, 128), ab_ref[1, KS - 1]), jnp.zeros((8, 128), F32)
-    for j in range(KS - 2, -1, -1):
-        tr, ti = rotated(tr, ti, ec, es)
-        tr = tr + ab_ref[1, j]
-    tr, ti = tr[0:1] * (1.0 / 512.0), ti[0:1] * (1.0 / 512.0)
-    ym = jnp.where(m >= G // 2, m - G, m).astype(F32)[0:1] * (0.5 / G)
-    ysq = ym * ym
-    ws = [wo[q, 0:1, :] for q in range(2)]
-    row64 = lax.broadcasted_iota(jnp.int32, (64, 128), 0)
-    lane64 = lax.broadcasted_iota(jnp.int32, (64, 128), 1)
-
     def step_one(i):
         xo = (x + 2) % 4
         return (
@@ -344,24 +401,15 @@
     def compute(i):
         for q in range(4):
             rows = slice(q * 64, q * 64 + 64)
-            l = (row64 + q * 64) * 16 + i
-            xl = jnp.where(l >= G // 2, l - G, l).astype(F32) * (0.5 / G)
-            rho = xl * xl + ysq
-            n = -rho / (1.0 + jnp.sqrt(1.0 - rho))
-            zre = zim = None
+            part = None
             for v in range(2):
                 h = hp[v, i]
-                pc = lax.dot_general(dm_ref[rows, :], h, NT, preferred_element_type=F32)
-                ps = lax.dot_general(dm_ref[256 + q * 64 : 320 + q * 64, :], h, NT, preferred_element_type=F32)
+                pc = lax.dot_general(dm[rows], h, NT, preferred_element_type=F32)
+                ps = lax.dot_general(dm[256 + q * 64 : 320 + q * 64], h, NT, preferred_element_type=F32)
                 dre = pc[:, :128] - ps[:, 128:]
                 dim = ps[:, :128] + pc[:, 128:]
-                c, s = cos_sin(ws[v] * n)
-                a, b = rotated(dre, dim, c, s)
-                zre, zim = (a, b) if zre is None else (zre + a, zim + b)
-            a, b = rotated(zre, zim, tr, ti)
-            cs = jnp.sum(jnp.where(lane64 == i, sr[rows], 0.0), axis=1, keepdims=True)
-            ss = jnp.sum(jnp.where(lane64 == i, si[rows], 0.0), axis=1, keepdims=True)
-            part = cs * a - ss * b
+                term = eq[v, i, 0, rows] * dre - eq[v, i, 1, rows] * dim
+                part = term if part is None else part + term
             for k in range(2):
                 pb[i, q // 2, (q % 2) * 2 + k] = part[k * 32 : k * 32 + 32]
 
@@ -412,22 +460,15 @@
         return 0
 
     lax.fori_loop(0, 16, drain, 0)
-    for c in rings:
+    for c in far:
         c.wait_send()
-    for g in range(4):
-        swap(g).wait_send()
-
-def constants():
-    k = np.arange(256)
-    a = 2 * np.pi * (np.outer(k, k) % 256) / 256
-    dm = np.concatenate([np.cos(a), np.sin(a)], axis=0)
-    b = 2 * np.pi * np.outer(np.arange(16), k) / G
-    return dm.astype(jnp.bfloat16), np.stack([np.cos(b), np.sin(b)]).astype(np.float32)
+    for h in range(2):
+        for g in range(4):
+            swap(h, g).wait_send()
+
 
 def local(visibility, target, offset, taps, w_plane):
-    dm, tw = constants()
     count = visibility.shape[1]
-    ab = jnp.stack([taps, lax.reduce_precision(taps, 8, 7)])
     dma = pltpu.SemaphoreType.DMA
     vmem = pl.BlockSpec(memory_space=pltpu.VMEM)
     smem = pl.BlockSpec(memory_space=pltpu.SMEM)
@@ -436,7 +477,7 @@
     halves = pl.pallas_call(
         kernel,
         out_shape=jax.ShapeDtypeStruct((1024, 128), F32),
-        in_specs=[smem, smem] + [vmem] * 5,
+        in_specs=[smem, smem] + [vmem] * 3,
         out_specs=vmem,
         scratch_shapes=[
             pltpu.VMEM((2, 4, 16, 128), F32),
@@ -446,6 +487,9 @@
             pltpu.VMEM((3072, 128), F32),
             pltpu.VMEM((2, 16, 256, 256), F32),
             pltpu.VMEM((2, 16, 256, 256), BF16),
+            pltpu.VMEM((2, 16, 2, 256, 128), F32),
+            pltpu.VMEM((512, 256), BF16),
+            pltpu.VMEM((2, 16, 256), F32),
             pltpu.VMEM((4, 4, 64, 128), F32),
             pltpu.VMEM((4, 8, 128), F32),
             pltpu.VMEM((4, 8, 128), F32),
@@ -459,14 +503,15 @@
             part,
             part,
         ]
-        + [dma((3,))] * 6
-        + [dma((4,))] * 2
+        + [dma((3,))] * 2
+        + [dma((2, 3))] * 2
+        + [dma((2, 4))] * 4
         + [dma] * 2
         + [dma((16, 2))] * 6
         + [dma((16,))] * 2,
         compiler_params=pltpu.CompilerParams(collective_id=0, has_side_effects=True, vmem_limit_bytes=56 << 20),
         name="dirtyimage",
-    )(w_plane, ab, visibility, target.reshape(1, count), offset.reshape(1, count), jnp.asarray(tw), jnp.asarray(dm))
+    )(w_plane, taps, visibility, target.reshape(1, count), offset.reshape(1, count))
     return jnp.concatenate([halves[:512], halves[512:]], axis=1)
 
 

time: 87.8 us -> 82.7 us (0.942)
  Pallas kernels: 83.8 us -> 80 us
    pallas_call x1, Pallas kernels: 83.8 us -> 80 us  [local(): pl.pallas_call(kernel, out_shape=jax.ShapeDtypeStruct((1024, 128), F32),...]
where the time goes in v4:
time: 82.7 us; the launch traced here: 82.5 us
  Pallas kernels  80 us (97%)
  local copies, waits for them, and re-layouts  1.07 us (1%)
  other arithmetic  0.83 us (1%)
    pallas_call x1, Pallas kernels, local(): pl.pallas_call(kernel, out_shape=jax.ShapeDtypeStruct((1024, 128), F32),...  80 us

profile of v4, /device:TPU:0, one launch (start us, length us, event | category | flops | bytes accessed | tf_op | source)
XLA Modules:
  0.0 82.5 jit_solution(3972832129636331291)
XLA Ops:
  0.7 80.0 %dirtyimage.1 = f32[1024,128]{1,0:T(8,128)} custom-call(f32[1]{0:T(128)S(6)} %copy.6.w_ref, f32[8]{0:T(128)} %taps_ref.1, f32[2,2048]{1,0:T(2,128)} %vis_ref.1, s32[1,2048]{1,0:T(1,128)} %bitcast.2, s32[1,2048]{1,0:T(1,128)} %bitcast.3), custom_call_target="tpu_custom_call" | custom-call | tf_op jit(solution)/shard_map/dirtyimage/pallas_call | solution.py:477
  80.6 1.1 %fusion = (f32[512,128]{1,0:T(8,128)S(1)}, f32[512,128]{1,0:T(8,128)S(1)}) fusion(f32[1024,128]{1,0:T(8,128)} %dirtyimage.1), kind=kLoop, calls=%fused_computation.1 | loop fusion | bytes 1048576 | tf_op jit(solution)/shard_map/slice | solution.py:515
  81.7 0.8 %pad_maximum_fusion = f32[512,256]{1,0:T(8,128)} fusion(f32[512,128]{1,0:T(8,128)S(1)} %get-tuple-element.6, f32[512,128]{1,0:T(8,128)S(1)} %get-tuple-element.5), kind=kLoop, calls=%fused_computation | loop fusion | flops 131072 | bytes 1048576 | tf_op jit(solution)/shard_map/concatenate | solution.py:515

commit v5 on v4

--- a/solution.py
+++ b/solution.py
@@ -10,6 +10,8 @@
 
 G = 4096
 KS = 8
+CHUNKS = 8
+SUB = 16 // CHUNKS
 MESH = pl.DeviceIdType.MESH
 F32 = jnp.float32
 BF16 = jnp.bfloat16
@@ -108,8 +110,8 @@
 
 
 def kernel(w_ref, taps_ref, vis_ref, tgt_ref, off_ref, out_ref, *scratch):
-    sb, wb, wo, ra, ga, hs, hp, eq, dm, tw, xs, ts, rs, sr, si, pb, r1, fw, rc, rd, zb, zr = scratch[:22]
-    sa, qa, sn, qn, sv, qv, sc, qc, sw, qw, s1, q1, sf, qf, sd, qd, sz, qz = scratch[22:]
+    sb, wb, wo, ra, ga, hs, hp, eq, dm, tw, xs, ts, rs, sr, si, pb, r1, fw, rc, zb, zr, oh = scratch[:22]
+    sa, qa, sn, qn, sv, qv, sc, qc, sw, qw, s1, q1, sf, qf, sz, qz = scratch[22:]
     zh, x, zl, y, core = place()
     z = zh * 2 + zl
     p, t = zh * 4 + x, zl * 8 + y * 2 + core
@@ -191,7 +193,7 @@
             eq[v, i, 1, rows] = s
         return 0
 
-    lax.fori_loop(0, 12, screen, 0)
+    lax.fori_loop(0, 10, screen, 0)
     for c in first:
         c.wait()
 
@@ -222,7 +224,7 @@
     for c in near:
         c.start()
     wcopy.wait()
-    lax.fori_loop(12, 24, screen, 0)
+    lax.fori_loop(10, 20, screen, 0)
     for q in range(8):
         a = lax.broadcasted_iota(jnp.int32, (32, 256), 0) + q * 32
         b = lax.broadcasted_iota(jnp.int32, (32, 256), 1)
@@ -334,10 +336,11 @@
         for h in range(2):
             arrival(h, g).wait_recv()
             swap(h, g).start()
-    lax.fori_loop(24, 32, screen, 0)
+    lax.fori_loop(20, 25, screen, 0)
     for h in range(2):
         arrival(h, 3).wait_recv()
         swap(h, 3).start()
+    lax.fori_loop(25, 32, screen, 0)
     for g in (1, 2, 3):
         for h in range(2):
             swapped(h, g).wait_recv()
@@ -379,70 +382,67 @@
     def step_one(i):
         xo = (x + 2) % 4
         return (
-            copy(pb.at[i, 0, xo], r1.at[i, 0], s1.at[i, 0], q1.at[i, 0], right),
-            copy(pb.at[i, 1, xo], r1.at[i, 1], s1.at[i, 1], q1.at[i, 1], left),
+            copy(pb.at[i, 0, xo], r1.at[i, 0], s1, q1.at[i, 0], right),
+            copy(pb.at[i, 1, xo], r1.at[i, 1], s1, q1.at[i, 1], left),
         )
 
-    def direct(i):
+    def step_two(i):
         return (
-            copy(pb.at[i, 0, xm], rd.at[i, 0], sd.at[i, 0], qd.at[i, 0], left),
-            copy(pb.at[i, 1, xp], rd.at[i, 1], sd.at[i, 1], qd.at[i, 1], right),
+            copy(fw.at[i, 0], rc.at[i, 0], sf, qf.at[i, 0], right),
+            copy(fw.at[i, 1], rc.at[i, 1], sf, qf.at[i, 1], left),
         )
 
-    def forward(i):
-        return (
-            copy(fw.at[i, 0], rc.at[i, 0], sf.at[i, 0], qf.at[i, 0], right),
-            copy(fw.at[i, 1], rc.at[i, 1], sf.at[i, 1], qf.at[i, 1], left),
-        )
-
     def over(i):
-        return copy(zb.at[i], zr.at[i], sz.at[i], qz.at[i], across)
+        return copy(zb.at[i], zr.at[i], sz, qz.at[i], across)
 
     def compute(i):
-        for q in range(4):
-            rows = slice(q * 64, q * 64 + 64)
-            part = None
-            for v in range(2):
-                h = hp[v, i]
-                pc = lax.dot_general(dm[rows], h, NT, preferred_element_type=F32)
-                ps = lax.dot_general(dm[256 + q * 64 : 320 + q * 64], h, NT, preferred_element_type=F32)
-                dre = pc[:, :128] - ps[:, 128:]
-                dim = ps[:, :128] + pc[:, 128:]
-                term = eq[v, i, 0, rows] * dre - eq[v, i, 1, rows] * dim
-                part = term if part is None else part + term
-            for k in range(2):
-                pb[i, q // 2, (q % 2) * 2 + k] = part[k * 32 : k * 32 + 32]
+        for k in range(SUB):
+            j = i * SUB + k
+            pair = [lax.dot_general(dm[...], hp[v, j], NT, preferred_element_type=F32) for v in range(2)]
+            for q in range(8):
+                rows = slice(q * 32, q * 32 + 32)
+                part = None
+                for v in range(2):
+                    pc, ps = pair[v][q * 32 : q * 32 + 32], pair[v][256 + q * 32 : 288 + q * 32]
+                    dre = pc[:, :128] - ps[:, 128:]
+                    dim = ps[:, :128] + pc[:, 128:]
+                    term = eq[v, j, 0, rows] * dre - eq[v, j, 1, rows] * dim
+                    part = term if part is None else part + term
+                pb[i, q // 4, q % 4, k] = part
 
     def put(i, half, value):
-        out_ref[pl.ds(half * 512 + i, 32, stride=16), :] = value
-
-    lag1, lag2, lag3 = 4, 8, 12
+        for k in range(SUB):
+            oh[pl.ds(half * 512 + i * SUB + k, 32, stride=16), :] = value[k]
+
+    lag1, lag2, lag3 = 4, 7, 9
 
     def turn(i, _):
-        @pl.when(i < 16)
+        @pl.when(i < CHUNKS)
         def _():
             compute(i)
-            for c in step_one(i) + direct(i):
+            for c in step_one(i):
                 c.start()
 
-        @pl.when(jnp.logical_and(i >= lag1, i < 16 + lag1))
+        @pl.when(jnp.logical_and(i >= lag1, i < CHUNKS + lag1))
         def _():
             j = i - lag1
             for c in step_one(j):
                 c.wait_recv()
-            fw[j, 0] = r1[j, 0] + pb[j, 0, xp]
-            fw[j, 1] = r1[j, 1] + pb[j, 1, xm]
-            for c in forward(j):
+            fw[j, 0, 0] = r1[j, 0] + pb[j, 0, xp]
+            fw[j, 0, 1] = pb[j, 1, xp]
+            fw[j, 1, 0] = pb[j, 0, xm]
+            fw[j, 1, 1] = r1[j, 1] + pb[j, 1, xm]
+            for c in step_two(j):
                 c.start()
 
-        @pl.when(jnp.logical_and(i >= lag2, i < 16 + lag2))
+        @pl.when(jnp.logical_and(i >= lag2, i < CHUNKS + lag2))
         def _():
             j = i - lag2
-            for c in forward(j) + direct(j):
+            for c in step_two(j):
                 c.wait_recv()
-            put(j, zh, pb[j, zh, x] + rc[j, zh] + rd[j, zh])
-            zb[j] = pb[j, 1 - zh, x] + rc[j, 1 - zh] + rd[j, 1 - zh]
+            zb[j] = pb[j, 1 - zh, x] + rc[j, 0, 1 - zh] + rc[j, 1, 1 - zh]
             over(j).start()
+            put(j, zh, pb[j, zh, x] + rc[j, 0, zh] + rc[j, 1, zh])
 
         @pl.when(i >= lag3)
         def _():
@@ -452,14 +452,12 @@
 
         return 0
 
-    lax.fori_loop(0, 16 + lag3, turn, 0)
-
-    def drain(i, _):
-        for c in step_one(i) + direct(i) + forward(i) + (over(i),):
-            c.wait_send()
-        return 0
-
-    lax.fori_loop(0, 16, drain, 0)
+    lax.fori_loop(0, CHUNKS + lag3, turn, 0)
+    out_ref[:, :128] = oh[:512]
+    out_ref[:, 128:] = oh[512:]
+    copy(r1, r1, s1, q1.at[0, 0], right).wait_send()
+    copy(fw, fw, sf, qf.at[0, 0], right).wait_send()
+    copy(zb, zb, sz, qz.at[0], right).wait_send()
     for c in far:
         c.wait_send()
     for h in range(2):
@@ -472,11 +470,11 @@
     dma = pltpu.SemaphoreType.DMA
     vmem = pl.BlockSpec(memory_space=pltpu.VMEM)
     smem = pl.BlockSpec(memory_space=pltpu.SMEM)
-    buf = pltpu.VMEM((16, 2, 32, 128), F32)
-    part = pltpu.VMEM((16, 32, 128), F32)
-    halves = pl.pallas_call(
+    pair = pltpu.VMEM((CHUNKS, 2, 2, SUB, 32, 128), F32)
+    part = pltpu.VMEM((CHUNKS, SUB, 32, 128), F32)
+    return pl.pallas_call(
         kernel,
-        out_shape=jax.ShapeDtypeStruct((1024, 128), F32),
+        out_shape=jax.ShapeDtypeStruct((512, 256), F32),
         in_specs=[smem, smem] + [vmem] * 3,
         out_specs=vmem,
         scratch_shapes=[
@@ -495,24 +493,23 @@
             pltpu.VMEM((4, 8, 128), F32),
             pltpu.VMEM((256, 128), F32),
             pltpu.VMEM((256, 128), F32),
-            pltpu.VMEM((16, 2, 4, 32, 128), F32),
-            buf,
-            buf,
-            buf,
-            buf,
+            pltpu.VMEM((CHUNKS, 2, 4, SUB, 32, 128), F32),
+            pltpu.VMEM((CHUNKS, 2, SUB, 32, 128), F32),
+            pair,
+            pair,
             part,
             part,
+            pltpu.VMEM((1024, 128), F32),
         ]
         + [dma((3,))] * 2
         + [dma((2, 3))] * 2
         + [dma((2, 4))] * 4
-        + [dma] * 2
-        + [dma((16, 2))] * 6
-        + [dma((16,))] * 2,
+        + [dma] * 3
+        + [dma((CHUNKS, 2)), dma] * 2
+        + [dma((CHUNKS,))],
         compiler_params=pltpu.CompilerParams(collective_id=0, has_side_effects=True, vmem_limit_bytes=56 << 20),
         name="dirtyimage",
     )(w_plane, taps, visibility, target.reshape(1, count), offset.reshape(1, count))
-    return jnp.concatenate([halves[:512], halves[512:]], axis=1)
 
 
 def solution(mesh):

time: 82.7 us -> 78.3 us (0.947)
  Pallas kernels: 80 us -> 75.4 us
  other arithmetic: 0.83 us -> 0 us
    pallas_call x1, Pallas kernels: 80 us -> 75.4 us  [local(): pl.pallas_call(kernel, out_shape=jax.ShapeDtypeStruct((512, 256), F32), i...]
    unnamed x0 -> x1, local copies, waits for them, and re-layouts: none -> 1.87 us
    slice x1 -> x0, local copies, waits for them, and re-layouts: 1.07 us -> none  [local(): return jnp.concatenate([halves[:512], halves[512:]], axis=1)]
    concatenate x1 -> x0, other arithmetic: 0.83 us -> none  [local(): return jnp.concatenate([halves[:512], halves[512:]], axis=1)]
where the time goes in v5:
time: 78.3 us; the launch traced here: 78 us
  Pallas kernels  75.4 us (96%)
  local copies, waits for them, and re-layouts  1.87 us (2%)
    pallas_call x1, Pallas kernels, local(): pl.pallas_call(kernel, out_shape=jax.ShapeDtypeStruct((512, 256), F32), i...  75.4 us
    unnamed x1, local copies, waits for them, and re-layouts  1.87 us

profile of v5, /device:TPU:0, one launch (start us, length us, event | category | flops | bytes accessed | tf_op | source)
XLA Modules:
  0.0 78.0 jit_solution(16202607816063592124)
XLA Ops:
  0.7 75.4 %dirtyimage.1 = f32[512,256]{1,0:T(8,128)} custom-call(f32[1]{0:T(128)S(6)} %copy.7.w_ref, f32[8]{0:T(128)} %taps_ref.1, f32[2,2048]{1,0:T(2,128)} %vis_ref.1, s32[1,2048]{1,0:T(1,128)} %bitcast.2, s32[1,2048]{1,0:T(1,128)} %bitcast.3), custom_call_target="tpu_custom_call" | custom-call | tf_op jit(solution)/shard_map/dirtyimage/pallas_call | solution.py:475
  76.1 1.9 %copy.8 = f32[512,256]{1,0:T(8,128)} copy(f32[512,256]{1,0:T(8,128)} %dirtyimage.1) | data formatting | bytes 1048576

commit v6 on v5

--- a/solution.py
+++ b/solution.py
@@ -10,8 +10,7 @@
 
 G = 4096
 KS = 8
-CHUNKS = 8
-SUB = 16 // CHUNKS
+CHUNKS, SUB = 8, 2
 MESH = pl.DeviceIdType.MESH
 F32 = jnp.float32
 BF16 = jnp.bfloat16
@@ -68,27 +67,29 @@
     return out_r, out_i
 
 
-def sort(vis_ref, tgt_ref, off_ref, out_ref):
-    count = tgt_ref.shape[1]
+def sort(in_ref, out_ref):
+    count = in_ref.shape[1]
     blk = 256
     ii = lax.broadcasted_iota(jnp.int32, (blk, blk), 0)
     jj = lax.broadcasted_iota(jnp.int32, (blk, blk), 1)
     tri = jnp.where(ii < jj, 1.0, 0.0).astype(BF16)
-    rows = lax.broadcasted_iota(jnp.int32, (128, blk), 0)
+    rows = lax.broadcasted_iota(jnp.int32, (128, blk), 0).astype(F32)
     ranks = lax.broadcasted_iota(jnp.int32, (32, blk), 0).astype(F32)
     carry = jnp.zeros((128, 1), F32)
     acc = jnp.zeros((128, 128), F32)
     for b in range(count // blk):
         sl = slice(b * blk, (b + 1) * blk)
-        one = jnp.where(rows == tgt_ref[:, sl], 1.0, 0.0)
+        one = jnp.where(rows == in_ref[2:3, sl], 1.0, 0.0)
         oneb = one.astype(BF16)
         before = jnp.dot(oneb, tri, preferred_element_type=F32)
         rank = jnp.sum(one * (before + carry), axis=0, keepdims=True)
         carry = carry + jnp.sum(one, axis=1, keepdims=True)
         hit = ranks == rank
-        off = off_ref[:, sl]
-        parts = [((off >> 12) << 12).astype(F32), (((off >> 4) & 255) << 4).astype(F32), (off & 15).astype(F32)]
-        left = [vis_ref[0:1, sl], vis_ref[1:2, sl]]
+        off = in_ref[3:4, sl]
+        high = jnp.floor(off * (1.0 / 4096.0)) * 4096.0
+        mid = jnp.floor((off - high) * (1.0 / 16.0)) * 16.0
+        parts = [high, mid, off - high - mid]
+        left = [in_ref[0:1, sl], in_ref[1:2, sl]]
         for k in range(3):
             cols = []
             for v in range(2):
@@ -109,7 +110,7 @@
     return p // 4, p % 4, t // 8, (t // 2) % 4, t % 2
 
 
-def kernel(w_ref, taps_ref, vis_ref, tgt_ref, off_ref, out_ref, *scratch):
+def kernel(in_ref, out_ref, *scratch):
     sb, wb, wo, ra, ga, hs, hp, eq, dm, tw, xs, ts, rs, sr, si, pb, r1, fw, rc, zb, zr, oh = scratch[:22]
     sa, qa, sn, qn, sv, qv, sc, qc, sw, qw, s1, q1, sf, qf, sz, qz = scratch[22:]
     zh, x, zl, y, core = place()
@@ -141,8 +142,24 @@
             src_ref=src, dst_ref=dst, send_sem=send, recv_sem=recv, device_id=device, device_id_type=MESH
         )
 
-    sort(vis_ref, tgt_ref, off_ref, sb)
-    wb[...] = jnp.full((8, 128), w_ref[0])
+    for q in range(8):
+        a = lax.broadcasted_iota(jnp.int32, (32, 256), 0) + q * 32
+        b = lax.broadcasted_iota(jnp.int32, (32, 256), 1)
+        c, s = cos_sin(((a * b) % 256).astype(F32) * (1.0 / 256.0))
+        dm[q * 32 : q * 32 + 32] = c.astype(BF16)
+        dm[256 + q * 32 : 288 + q * 32] = s.astype(BF16)
+    a = lax.broadcasted_iota(jnp.int32, (16, 256), 0)
+    b = lax.broadcasted_iota(jnp.int32, (16, 256), 1)
+    c, s = cos_sin((a * b).astype(F32) * (1.0 / G))
+    tw[0] = c
+    tw[1] = s
+    sort(in_ref, sb)
+    small = in_ref[4:5, 0:128]
+
+    def spread(n, shape):
+        return jnp.broadcast_to(small[:, n : n + 1], shape)
+
+    wb[...] = spread(KS, (8, 128))
     wo[zh] = wb[...]
     pl.semaphore_wait(barrier, 10)
     first = [copy(sb.at[:, (x + d) % 4], ra.at[x], sa.at[d - 1], qa.at[d - 1], at_x(d)) for d in (1, 3, 2)]
@@ -155,15 +172,15 @@
     l0 = lax.broadcasted_iota(jnp.int32, (256, 128), 0)
     lane = lax.broadcasted_iota(jnp.int32, (256, 128), 1)
     ec, es = cos_sin((l0 * 16 + lane).astype(F32) * (1.0 / G))
-    ar, ai = jnp.full((256, 128), taps_ref[KS - 1]), jnp.zeros((256, 128), F32)
+    ar, ai = spread(KS - 1, (256, 128)), jnp.zeros((256, 128), F32)
     for j in range(KS - 2, -1, -1):
         ar, ai = rotated(ar, ai, ec, es)
-        ar = ar + taps_ref[j]
+        ar = ar + spread(j, (256, 128))
     sr[...] = ar
     si[...] = ai
     m = t * 256 + zh * 128 + lax.broadcasted_iota(jnp.int32, (8, 128), 1)
     ec, es = cos_sin(m.astype(F32) * (1.0 / G))
-    taps_low = [jnp.full((8, 128), taps_ref[j]).astype(BF16).astype(F32) for j in range(KS)]
+    taps_low = [spread(j, (8, 128)).astype(BF16).astype(F32) for j in range(KS)]
     tr, ti = taps_low[KS - 1], jnp.zeros((8, 128), F32)
     for j in range(KS - 2, -1, -1):
         tr, ti = rotated(tr, ti, ec, es)
@@ -193,7 +210,7 @@
             eq[v, i, 1, rows] = s
         return 0
 
-    lax.fori_loop(0, 10, screen, 0)
+    lax.fori_loop(0, 13, screen, 0)
     for c in first:
         c.wait()
 
@@ -224,18 +241,7 @@
     for c in near:
         c.start()
     wcopy.wait()
-    lax.fori_loop(10, 20, screen, 0)
-    for q in range(8):
-        a = lax.broadcasted_iota(jnp.int32, (32, 256), 0) + q * 32
-        b = lax.broadcasted_iota(jnp.int32, (32, 256), 1)
-        c, s = cos_sin(((a * b) % 256).astype(F32) * (1.0 / 256.0))
-        dm[q * 32 : q * 32 + 32] = c.astype(BF16)
-        dm[256 + q * 32 : 288 + q * 32] = s.astype(BF16)
-    a = lax.broadcasted_iota(jnp.int32, (16, 256), 0)
-    b = lax.broadcasted_iota(jnp.int32, (16, 256), 1)
-    c, s = cos_sin((a * b).astype(F32) * (1.0 / G))
-    tw[0] = c
-    tw[1] = s
+    lax.fori_loop(13, 28, screen, 0)
     for c in near:
         c.wait()
 
@@ -316,69 +322,82 @@
         tab, hot = jnp.concatenate(tabs, axis=1), jnp.concatenate(hots, axis=1)
         return lax.dot_general(tab, hot, NT, preferred_element_type=F32)
 
-    def early(h, _):
-        start = start_of(h, 0)
-
-        def quad(it, _):
-            for u in range(4):
-                dense(start + it * 4 + u, u)
-            for u in range(4):
-                hs[h, it * 4 + u] = total([u])
-            return 0
-
-        lax.fori_loop(0, 4, quad, 0)
+    def fill(h, g, it):
+        for u in range(4):
+            dense(start_of(h, g) + it * 4 + u, u)
+
+    def early(n, _):
+        h, it = n // 4, n % 4
+        fill(h, 0, it)
+        for u in range(4):
+            hs[h, it * 4 + u] = total([u])
         return 0
 
     for h in range(2):
         swapped(h, 0).wait_recv()
-    lax.fori_loop(0, 2, early, 0)
-    for g in (1, 2):
-        for h in range(2):
-            arrival(h, g).wait_recv()
-            swap(h, g).start()
-    lax.fori_loop(20, 25, screen, 0)
+    lax.fori_loop(0, 8, early, 0)
     for h in range(2):
-        arrival(h, 3).wait_recv()
-        swap(h, 3).start()
-    lax.fori_loop(25, 32, screen, 0)
-    for g in (1, 2, 3):
-        for h in range(2):
-            swapped(h, g).wait_recv()
-
-    def late(h, _):
-        starts = [start_of(h, g) for g in (1, 2, 3)]
-        for u in range(3):
-            dense(starts[u], u)
-
-        def one(band, _):
-            hs[h, band] += total([0, 1, 2])
-            following = jnp.minimum(band + 1, 15)
-            for u in range(3):
-                dense(starts[u] + following, u)
+        arrival(h, 1).wait_recv()
+        swap(h, 1).start()
+    lax.fori_loop(28, 32, screen, 0)
+
+    def late(n, _):
+        g, h, it = 1 + n // 8, n // 4 % 2, n % 4
+
+        @pl.when(n % 8 == 0)
+        def _():
+            for k in range(2):
+                swapped(k, g).wait_recv()
+
+        @pl.when(n == 3)
+        def _():
+            for f in (2, 3):
+                for k in range(2):
+                    arrival(k, f).wait_recv()
+                    swap(k, f).start()
+
+        fill(h, g, it)
+        for u in range(4):
+            hs[h, it * 4 + u] += total([u])
+        return 0
+
+    lax.fori_loop(0, 24, late, 0)
+
+    def strip(rho):
+        def some(i, _):
+            v = i // 8
+            m = pl.multiple_of(i % 8 * 16, 16)
+            for h in range(2):
+                lanes = slice(h * 128, h * 128 + 128)
+                outs_r, outs_i = [], []
+                for b in range(4):
+                    r = [hs[v, b + 4 * k, pl.ds(m, 16), lanes] for k in range(4)]
+                    q = [hs[v, b + 4 * k, pl.ds(m + 128, 16), lanes] for k in range(4)]
+                    if rho % 2 == 0:
+                        er, ei, dr, di = r[0] + r[2], q[0] + q[2], r[1] + r[3], q[1] + q[3]
+                        yr, yi = (er + dr, ei + di) if rho == 0 else (er - dr, ei - di)
+                    else:
+                        er, ei, dr, di = r[0] - r[2], q[0] - q[2], r[1] - r[3], q[1] - q[3]
+                        yr, yi = (er - di, ei + dr) if rho == 1 else (er + di, ei - dr)
+                    if b and rho:
+                        turn = 2 * math.pi * b * rho / 16
+                        yr, yi = rotated(yr, yi, math.cos(turn), math.sin(turn))
+                    outs_r.append(yr)
+                    outs_i.append(yi)
+                outs_r, outs_i = dft(outs_r, outs_i)
+                for k in range(4):
+                    c, d, j = outs_r[k], outs_i[k], rho + 4 * k
+                    if j:
+                        c, d = rotated(c, d, tw[0, j : j + 1, lanes], tw[1, j : j + 1, lanes])
+                    hp[v, j, pl.ds(m, 16), lanes] = c.astype(BF16)
+                    hp[v, j, pl.ds(m + 128, 16), lanes] = d.astype(BF16)
             return 0
 
-        lax.fori_loop(0, 16, one, 0)
-        return 0
-
-    lax.fori_loop(0, 2, late, 0)
-
-    def strip(i, _):
-        v = i // 8
-        m = pl.multiple_of(i % 8 * 16, 16)
-        for h in range(2):
-            lanes = slice(h * 128, h * 128 + 128)
-            re = [hs[v, b, pl.ds(m, 16), lanes] for b in range(16)]
-            im = [hs[v, b, pl.ds(m + 128, 16), lanes] for b in range(16)]
-            re, im = dft(re, im)
-            for q in range(16):
-                a, b = re[q], im[q]
-                if q:
-                    a, b = rotated(a, b, tw[0, q : q + 1, lanes], tw[1, q : q + 1, lanes])
-                hp[v, q, pl.ds(m, 16), lanes] = a.astype(BF16)
-                hp[v, q, pl.ds(m + 128, 16), lanes] = b.astype(BF16)
-        return 0
-
-    lax.fori_loop(0, 16, strip, 0)
+        return some
+
+    def row_class(i, k):
+        return i // 2 + 4 * (i % 2 * 2 + k)
+
     def step_one(i):
         xo = (x + 2) % 4
         return (
@@ -397,7 +416,7 @@
 
     def compute(i):
         for k in range(SUB):
-            j = i * SUB + k
+            j = row_class(i, k)
             pair = [lax.dot_general(dm[...], hp[v, j], NT, preferred_element_type=F32) for v in range(2)]
             for q in range(8):
                 rows = slice(q * 32, q * 32 + 32)
@@ -412,11 +431,17 @@
 
     def put(i, half, value):
         for k in range(SUB):
-            oh[pl.ds(half * 512 + i * SUB + k, 32, stride=16), :] = value[k]
-
-    lag1, lag2, lag3 = 4, 7, 9
+            oh[pl.ds(half * 512 + row_class(i, k), 32, stride=16), :] = value[k]
+
+    lag1, lag2, lag3 = 2, 5, 7
 
     def turn(i, _):
+        for rho in range(4):
+
+            @pl.when(i == 2 * rho)
+            def _():
+                lax.fori_loop(0, 16, strip(rho), 0)
+
         @pl.when(i < CHUNKS)
         def _():
             compute(i)
@@ -469,13 +494,15 @@
     count = visibility.shape[1]
     dma = pltpu.SemaphoreType.DMA
     vmem = pl.BlockSpec(memory_space=pltpu.VMEM)
-    smem = pl.BlockSpec(memory_space=pltpu.SMEM)
+    small = jnp.concatenate([taps, w_plane, jnp.zeros((count - KS - 1,), F32)])
+    rows = [visibility, target.reshape(1, count).astype(F32), offset.reshape(1, count).astype(F32)]
+    packed = jnp.concatenate(rows + [small.reshape(1, count), jnp.zeros((3, count), F32)], axis=0)
     pair = pltpu.VMEM((CHUNKS, 2, 2, SUB, 32, 128), F32)
     part = pltpu.VMEM((CHUNKS, SUB, 32, 128), F32)
     return pl.pallas_call(
         kernel,
         out_shape=jax.ShapeDtypeStruct((512, 256), F32),
-        in_specs=[smem, smem] + [vmem] * 3,
+        in_specs=[vmem],
         out_specs=vmem,
         scratch_shapes=[
             pltpu.VMEM((2, 4, 16, 128), F32),
@@ -507,9 +534,9 @@
         + [dma] * 3
         + [dma((CHUNKS, 2)), dma] * 2
         + [dma((CHUNKS,))],
-        compiler_params=pltpu.CompilerParams(collective_id=0, has_side_effects=True, vmem_limit_bytes=56 << 20),
+        compiler_params=pltpu.CompilerParams(collective_id=0, has_side_effects=True, vmem_limit_bytes=36 << 20),
         name="dirtyimage",
-    )(w_plane, taps, visibility, target.reshape(1, count), offset.reshape(1, count))
+    )(packed)
 
 
 def solution(mesh):

time: 78.3 us -> 75.8 us (0.968)
  Pallas kernels: 75.4 us -> 71.8 us
    pallas_call x1, Pallas kernels: 75.4 us -> 71.8 us  [local(): pl.pallas_call(kernel, out_shape=jax.ShapeDtypeStruct((512, 256), F32), i...]
    unnamed x1 -> x7, local copies, waits for them, and re-layouts: 1.87 us -> 2.15 us
where the time goes in v6:
time: 75.8 us; the launch traced here: 75.5 us
  Pallas kernels  71.8 us (95%)
  local copies, waits for them, and re-layouts  2.32 us (3%)
    pallas_call x1, Pallas kernels, local(): pl.pallas_call(kernel, out_shape=jax.ShapeDtypeStruct((512, 256), F32), i...  71.8 us
    unnamed x7, local copies, waits for them, and re-layouts  2.15 us

profile of v6, /device:TPU:0, one launch (start us, length us, event | category | flops | bytes accessed | tf_op | source)
XLA Modules:
  0.0 75.5 jit_solution(11707744686679977968)
XLA Ops:
  0.7 0.0 copy-start.1
  0.7 0.7 convert_bitcast_fusion
  1.4 0.0 copy-done.1
  1.4 0.0 copy-start.2
  1.4 0.6 copy-done.2
  2.0 0.1 concatenate.6
  2.1 0.0 copy-start
  2.1 0.7 copy-done
  2.8 0.1 concatenate.7.in_ref
  2.9 71.8 %dirtyimage.1 = f32[512,256]{1,0:T(8,128)S(1)} custom-call(f32[8,2048]{1,0:T(8,128)S(1)} %concatenate.7.in_ref), custom_call_target="tpu_custom_call" | custom-call | tf_op jit(solution)/shard_map/dirtyimage/pallas_call | solution.py:502
  74.7 0.8 %copy.8 = f32[512,256]{1,0:T(8,128)} copy(f32[512,256]{1,0:T(8,128)S(1)} %dirtyimage.1) | data formatting | bytes 1048576
  (3 shorter events, 0.0 us)
Async XLA Ops:
  0.7 0.7 copy-start.1
  1.4 0.7 copy-start.2
  2.1 0.7 copy-start

commit v7 on v6

--- a/solution.py
+++ b/solution.py
@@ -448,6 +448,15 @@
             for c in step_one(i):
                 c.start()
 
+        @pl.when(jnp.logical_and(i >= lag2, i < CHUNKS + lag2))
+        def _():
+            j = i - lag2
+            for c in step_two(j):
+                c.wait_recv()
+            zb[j] = pb[j, 1 - zh, x] + rc[j, 0, 1 - zh] + rc[j, 1, 1 - zh]
+            over(j).start()
+            put(j, zh, pb[j, zh, x] + rc[j, 0, zh] + rc[j, 1, zh])
+
         @pl.when(jnp.logical_and(i >= lag1, i < CHUNKS + lag1))
         def _():
             j = i - lag1
@@ -459,15 +468,6 @@
             fw[j, 1, 1] = r1[j, 1] + pb[j, 1, xm]
             for c in step_two(j):
                 c.start()
-
-        @pl.when(jnp.logical_and(i >= lag2, i < CHUNKS + lag2))
-        def _():
-            j = i - lag2
-            for c in step_two(j):
-                c.wait_recv()
-            zb[j] = pb[j, 1 - zh, x] + rc[j, 0, 1 - zh] + rc[j, 1, 1 - zh]
-            over(j).start()
-            put(j, zh, pb[j, zh, x] + rc[j, 0, zh] + rc[j, 1, zh])
 
         @pl.when(i >= lag3)
         def _():

time: 75.8 us -> 75.8 us (level)
  no operation moved by 1% of the time
where the time goes in v7:
time: 75.8 us; the launch traced here: 75.5 us
  Pallas kernels  71.8 us (95%)
  local copies, waits for them, and re-layouts  2.32 us (3%)
    pallas_call x1, Pallas kernels, local(): pl.pallas_call(kernel, out_shape=jax.ShapeDtypeStruct((512, 256), F32), i...  71.8 us
    unnamed x7, local copies, waits for them, and re-layouts  2.15 us

profile of v7, /device:TPU:0, one launch (start us, length us, event | category | flops | bytes accessed | tf_op | source)
XLA Modules:
  0.0 75.5 jit_solution(9623469129158372424)
XLA Ops:
  0.7 0.0 copy-start.1
  0.7 0.7 convert_bitcast_fusion
  1.4 0.0 copy-done.1
  1.4 0.0 copy-start.2
  1.4 0.6 copy-done.2
  2.0 0.1 concatenate.6
  2.1 0.0 copy-start
  2.1 0.7 copy-done
  2.8 0.1 concatenate.7.in_ref
  2.9 71.8 %dirtyimage.1 = f32[512,256]{1,0:T(8,128)S(1)} custom-call(f32[8,2048]{1,0:T(8,128)S(1)} %concatenate.7.in_ref), custom_call_target="tpu_custom_call" | custom-call | tf_op jit(solution)/shard_map/dirtyimage/pallas_call | solution.py:502
  74.7 0.8 %copy.8 = f32[512,256]{1,0:T(8,128)} copy(f32[512,256]{1,0:T(8,128)S(1)} %dirtyimage.1) | data formatting | bytes 1048576
  (3 shorter events, 0.0 us)
Async XLA Ops:
  0.7 0.7 copy-start.1
  1.4 0.7 copy-start.2
  2.1 0.7 copy-start
